TPU v7x, 256 devices: a whole 4x4x8 slice. The times are simulated.
256 devices in a mesh: comp: 2 (over z_hi), lat: 8 (over z_lo, core), lon: 16 (over y, x).
Axes of the slice: x: 4, y: 4, z: 8 (z_hi: 2, z_lo: 4; z = z_hi * 4 + z_lo), core: 2. Of those that a mesh axis runs over, the one named last changes fastest.
Arguments:
- fields: float32 [2, 7, 16384, 256], P('comp', None, ('lat', 'lon')), may hold values from -4 to 4, as said below
- block_owner: int32 [16384], P(('lat', 'lon')), may hold values from 0 to 16383, as said below
- ice_covered: int32 [16384], P(('lat', 'lon')), may hold values 0 or 1
- land_mask: int32 [16384, 256], P(('lat', 'lon')), may hold values 0 or 1
Outputs:
- coupled_out: float32 [2, 2, 16384, 256], P('comp', None, ('lat', 'lon'))
Inputs may be any that keep to these rules, and one draw needn't show every extreme that they name: `block_owner`: every block id appears once. Slot d of lat+lon index o holds a block of the ice tile of index d, that is an id from d * 128 to d * 128 + 127. `fields`: ocean channels: winds within 4, currents within 1.5, tilts within 1, air density 0.9 to 1.3; ice channels: velocities within 1.5, mass 0.5 to 4, concentration 0.05 to 1, stresses within 1.5.
All inputs are finite; a program needn't handle non-finite values.
Results may differ from a plain program's by a relative error of at most 0.00002.
Values sent between devices are 32-bit elements.
A program may use at most 64 MiB of HBM per device.

v0:
```python
import jax
import jax.numpy as jnp
from jax import lax
from jax.sharding import PartitionSpec as P

GX = 1
BY = 2
BX = 128
NSUB = 4


CD_ICE = 0.1
CW = 1.5
CSTAR = 2.0
ECC2 = 4.0
DMIN2 = 0.25
RELAX = 0.5
DTE = 0.5
CORIO = 0.3
MASS_FLOOR = 0.5
DRAG_FLOOR = 0.1


def in_blocks(x, dim, size):
    before, after = (x.shape[:dim], x.shape[dim + 1 :])
    return jnp.moveaxis(x.reshape(*before, size, -1, *after), dim, 0)


def in_order(tiles, dim):
    lengths = list(tiles.shape[1:])
    lengths[dim] *= tiles.shape[0]
    return jnp.moveaxis(tiles, 0, dim).reshape(lengths)


def exchange_both(x, axis, axes, splits, concats):
    sizes = [lax.axis_size(a) for a in axes]
    tiles = in_blocks(x, splits[0], sizes[0])
    tiles = jnp.moveaxis(in_blocks(tiles, splits[1] + 1, sizes[1]), 0, 1)
    inside = tiles.shape[2:]
    tiles = tiles.reshape(-1, *inside)
    tiles = lax.all_to_all(tiles, axis, split_axis=0, concat_axis=0, tiled=True)
    tiles = in_order(tiles.reshape(*sizes, *inside), concats[0] + 1)
    return in_order(tiles, concats[1])


def with_halo(x, sides, width, wrap):
    for axis, dim in sides:
        size, length = (lax.axis_size(axis), x.shape[dim])
        up = [(i, (i + 1) % size) for i in range(size if wrap else size - 1)]
        down = [(j, i) for i, j in up]
        last = lax.slice_in_dim(x, length - width, length, axis=dim)
        first = lax.slice_in_dim(x, 0, width, axis=dim)
        before = lax.ppermute(last, axis, up)
        after = lax.ppermute(first, axis, down)
        x = jnp.concatenate([before, x, after], axis=dim)
    return x


def air_stress(ocean):
    wind_x, wind_y, current_x, current_y, tilt_x, tilt_y, density = ocean
    speed_ice = jnp.sqrt(wind_x * wind_x + wind_y * wind_y + 1.0)
    scale_ice = density * CD_ICE * speed_ice
    rel_x = wind_x - current_x
    rel_y = wind_y - current_y
    speed_open = jnp.sqrt(rel_x * rel_x + rel_y * rel_y + 1.0)
    scale_open = density * (0.1 + 0.05 * speed_open) * speed_open
    outbound = jnp.stack(
        [scale_ice * wind_x, scale_ice * wind_y, current_x, current_y, tilt_x, tilt_y]
    )
    open_stress = jnp.stack([scale_open * rel_x, scale_open * rel_y])
    return (outbound, open_stress)


def prepare(ice_tile, forcing, active):
    ice_mass = ice_tile[2]
    concentration = ice_tile[3]
    strength = ice_mass * jnp.exp(CSTAR * (concentration - 1.0)) * active
    drag_base = CW * concentration * active
    push_x = active * (concentration * forcing[0] - ice_mass * forcing[4])
    push_y = active * (concentration * forcing[1] - ice_mass * forcing[5])
    return jnp.stack(
        [strength, ice_mass, drag_base, push_x, push_y, forcing[2], forcing[3], active]
    )


def subcycle(ice_state, statics):
    east_vel, north_vel, stress_one, stress_two, stress_three = ice_state
    strength = statics[0]
    east_base = east_vel[:-1, :-1]
    north_base = north_vel[:-1, :-1]
    strain_xx = east_vel[:-1, 1:] - east_base
    strain_yy = north_vel[1:, :-1] - north_base
    shear = east_vel[1:, :-1] - east_base + (north_vel[:-1, 1:] - north_base)
    divergence = strain_xx + strain_yy
    tension = strain_xx - strain_yy
    delta_norm = jnp.sqrt(
        divergence * divergence + (tension * tension + shear * shear) / ECC2 + DMIN2
    )
    viscosity = strength[:-1, :-1] / delta_norm
    stress_sum = (stress_one[:-1, :-1] + RELAX * viscosity * (divergence - delta_norm)) / (
        1.0 + RELAX
    )
    stress_diff = (stress_two[:-1, :-1] + RELAX * viscosity * tension / ECC2) / (1.0 + RELAX)
    stress_shear = (stress_three[:-1, :-1] + RELAX * viscosity * shear / (2.0 * ECC2)) / (
        1.0 + RELAX
    )
    stress_xx = 0.5 * (stress_sum + stress_diff)
    stress_yy = 0.5 * (stress_sum - stress_diff)
    force_x = (
        stress_xx[1:, 1:] - stress_xx[1:, :-1] + (stress_shear[1:, 1:] - stress_shear[:-1, 1:])
    )
    force_y = (
        stress_shear[1:, 1:] - stress_shear[1:, :-1] + (stress_yy[1:, 1:] - stress_yy[:-1, 1:])
    )
    trimmed = statics[:, 1:-1, 1:-1]
    strength, ice_mass, drag_base, push_x, push_y, current_x, current_y, active = trimmed
    east_old = east_vel[1:-1, 1:-1]
    north_old = north_vel[1:-1, 1:-1]
    diff_x = current_x - east_old
    diff_y = current_y - north_old
    drag_coef = drag_base * jnp.sqrt(diff_x * diff_x + diff_y * diff_y + DRAG_FLOOR)
    denominator = jnp.maximum(ice_mass, MASS_FLOOR) / DTE + drag_coef
    east_new = (
        active
        * (
            ice_mass / DTE * east_old
            + force_x
            + push_x
            + drag_coef * current_x
            + CORIO * ice_mass * north_old
        )
        / denominator
    )
    north_new = (
        active
        * (
            ice_mass / DTE * north_old
            + force_y
            + push_y
            + drag_coef * current_y
            - CORIO * ice_mass * east_old
        )
        / denominator
    )
    new_state = jnp.stack(
        [east_new, north_new, stress_sum[1:, 1:], stress_diff[1:, 1:], stress_shear[1:, 1:]]
    )
    return (new_state, trimmed)


def give_back(ice_state, statics):
    east_vel = ice_state[0]
    north_vel = ice_state[1]
    drag_base = statics[2]
    current_x = statics[5]
    current_y = statics[6]
    diff_x = east_vel - current_x
    diff_y = north_vel - current_y
    factor = drag_base * jnp.sqrt(diff_x * diff_x + diff_y * diff_y + DRAG_FLOOR)
    return jnp.stack([factor * diff_x, factor * diff_y, drag_base / CW])


def to_tile(blocks):
    channels, count, cells = blocks.shape
    arranged = blocks.reshape(channels, count // GX, GX, BY, BX).transpose(0, 1, 3, 2, 4)
    return arranged.reshape(channels, count // GX * BY, GX * BX)


def from_tile(values):
    channels, rows, columns = values.shape
    arranged = values.reshape(channels, rows // BY, BY, GX, BX).transpose(0, 1, 3, 2, 4)
    return arranged.reshape(channels, rows // BY * GX, BY * BX)


def per_device(fields, block_owner, ice_covered, land_mask):
    count = block_owner.shape[0]
    is_ocean = lax.axis_index("comp") == 0
    outbound, open_stress = air_stress(fields[0])
    owner_row = block_owner.reshape(1, count)
    paired = jnp.stack([outbound, outbound])
    owner_pair = jnp.stack([owner_row, owner_row])
    moved, moved_ids = (
        exchange_both(paired, ("comp", "lat", "lon"), ("comp", ("lat", "lon")), (0, 2), (0, 2)),
        exchange_both(owner_pair, ("comp", "lat", "lon"), ("comp", ("lat", "lon")), (0, 2), (0, 2)),
    )
    received = moved[0]
    anchor = moved_ids[0]
    local_ids = anchor[0] % count
    position = jnp.zeros((count,), jnp.int32).at[local_ids].set(jnp.arange(count, dtype=jnp.int32))
    forcing = to_tile(received[:, position])
    ice_tile = to_tile(fields[0])
    covered = ice_covered.astype(jnp.float32)[:, None] * (1 - land_mask).astype(jnp.float32)
    active = to_tile(covered[None])[0]
    statics = prepare(ice_tile, forcing, active)
    ice_state = jnp.stack([ice_tile[0], ice_tile[1], ice_tile[4], ice_tile[5], ice_tile[6]])
    joined = jnp.concatenate([ice_state, statics], 0)
    joined = with_halo(joined, (("lon", 2),), NSUB, True)
    joined = with_halo(joined, (("lat", 1),), NSUB, False)
    ice_state = joined[:5]
    statics = joined[5:]
    for repeat in range(NSUB):
        ice_state, statics = subcycle(ice_state, statics)
    returned = from_tile(give_back(ice_state, statics))
    back_send = returned[:, local_ids]
    back_pair = jnp.stack([back_send, back_send])
    returned_pair = exchange_both(
        back_pair, ("comp", "lat", "lon"), ("comp", ("lat", "lon")), (0, 2), (0, 2)
    )
    received_back = returned_pair[1]
    ocean_out = received_back[:2] + (1.0 - received_back[2]) * open_stress
    ice_out = from_tile(ice_state[:2])
    return jnp.where(is_ocean, ocean_out, ice_out)[None]


def solution(mesh):
    placed = (
        P("comp", None, ("lat", "lon"), None),
        P(("lat", "lon")),
        P(("lat", "lon")),
        P(("lat", "lon"), None),
    )
    return jax.shard_map(
        per_device,
        mesh=mesh,
        in_specs=placed,
        out_specs=P("comp", None, ("lat", "lon"), None),
        check_vma=False,
    )
```

profile of v0, /device:TPU:65, one launch (start us, length us, event | category | flops | bytes accessed | tf_op | source)
XLA Modules:
  0.0 162.1 jit_solution(11778648298411702238)
XLA Ops:
  1.6 14.5 %all-to-all-start.1 = ((s32[256,1,1,1]{3,2,1,0:T(1,128)}), s32[256,1,1,1]{3,2,1,0:T(1,128)S(1)}, u32[]{:S(2)}, u32[]{:S(2)}) async-start(s32[256,1,1,1]{3,2,1,0:T(1,128)} %copy.145), calls=%async_computation.1 | async-start | bytes 262144 | tf_op jit(solution)/shard_map/all_to_all | solution.py:41
  16.1 1.1 fusion.88
  17.2 1.1 fusion.87
  19.6 2.8 %copy.141 = f32[256,1,6,1,256]{4,3,2,1,0:T(1,128)} copy(f32[256,1,6,1,256]{4,0,2,3,1:T(8,128)S(1)} %bitcast.359) | data formatting | bytes 3145728 | tf_op jit(solution)/shard_map/reshape | solution.py:40
  22.4 4.7 %all-to-all-done.1 = s32[256,1,1,1]{3,2,1,0:T(1,128)S(1)} async-done(((s32[256,1,1,1]{3,2,1,0:T(1,128)}), s32[256,1,1,1]{3,2,1,0:T(1,128)S(1)}, u32[]{:S(2)}, u32[]{:S(2)}) %all-to-all-start.1) | async-done | bytes 1056 | tf_op jit(solution)/shard_map/all_to_all | solution.py:41
  27.1 9.0 %all-to-all-start = ((f32[256,1,6,1,256]{4,3,2,1,0:T(1,128)}), f32[256,1,6,1,256]{4,3,2,1,0:T(1,128)S(1)}, u32[]{:S(2)}, u32[]{:S(2)}) async-start(f32[256,1,6,1,256]{4,3,2,1,0:T(1,128)} %copy.141), calls=%async_computation | async-start | bytes 3145728 | tf_op jit(solution)/shard_map/all_to_all | solution.py:41
  43.0 0.9 constant_dynamic-update-slice_fusion.8
  48.6 1.0 copy.146
  49.6 1.0 scatter_custom_fusion
  50.6 27.1 %all-to-all-done = f32[256,1,6,1,256]{4,3,2,1,0:T(1,128)S(1)} async-done(((f32[256,1,6,1,256]{4,3,2,1,0:T(1,128)}), f32[256,1,6,1,256]{4,3,2,1,0:T(1,128)S(1)}, u32[]{:S(2)}, u32[]{:S(2)}) %all-to-all-start) | async-done | bytes 1572896 | tf_op jit(solution)/shard_map/all_to_all | solution.py:41
  78.9 1.8 %gather_fusion = f32[128,6,256]{2,1,0:T(8,128)} fusion(f32[6,128,256]{2,0,1:T(8,128)S(1)} %slice_bitcast_fusion, s32[1024]{0:T(1024)S(1)} %get-tuple-element.62), kind=kCustom, calls=%fused_computation | custom fusion | bytes 1573376 | tf_op jit(solution)/shard_map/gather | solution.py:190
  80.6 4.4 %fusion.120 = (f32[1,128,256]{2,0,1:T(1,128)S(1)}, f32[1,128,256]{2,0,1:T(1,128)S(1)}, f32[1,128,256]{2,0,1:T(1,128)S(1)}, f32[1,128,256]{2,0,1:T(1,128)S(1)}, f...) fusion(f32[6,128,256]{2,0,1:T(8,128)} %bitcast.364), kind=kLoop, calls=%fused_computation.253 | loop fusion | bytes 1572864 | tf_op jit(solution)/shard_map/slice | solution.py:80
  86.5 0.9 multiply_dynamic-update-slice_fusion.1
  87.7 1.5 collective-permute-start
  89.1 1.5 collective-permute-done.1
  90.7 3.4 %collective-permute-done = f32[13,256,4]{1,2,0:T(4,128)S(1)} collective-permute-done((f32[13,256,4]{1,2,0:T(4,128)S(1)}, f32[13,256,4]{1,2,0:T(4,128)S(1)}, u32[]{:S(2)}, u32[]{:S(2)}) %collective-permute-start) | collective-permute-done | bytes 53280 | tf_op jit(solution)/shard_map/ppermute | solution.py:53
  95.0 1.1 copy.167
  96.1 5.0 %collective-permute-start.3 = (f32[13,4,136]{2,1,0:T(4,128)}, f32[13,4,136]{2,1,0:T(4,128)S(1)}, u32[]{:S(2)}, u32[]{:S(2)}) collective-permute-start(f32[13,4,136]{2,1,0:T(4,128)} %copy.167), channel_id=1, source_target_pairs={{16,0},{32,16},{48,32},{64,48},{80,64},{96,80},{112,96},{17,1},{33... | collective-permute-start | bytes 84872 | tf_op jit(solution)/shard_map/ppermute | solution.py:54
  101.7 3.2 %collective-permute-start.2 = (f32[13,4,136]{2,1,0:T(4,128)S(1)}, f32[13,4,136]{2,1,0:T(4,128)}, u32[]{:S(2)}, u32[]{:S(2)}) collective-permute-start(f32[13,4,136]{2,1,0:T(4,128)S(1)} %copy.166), channel_id=1, source_target_pairs={{0,16},{16,32},{32,48},{48,64},{64,80},{80,96},{96,112},{1,17},{17... | collective-permute-start | bytes 84872 | tf_op jit(solution)/shard_map/ppermute | solution.py:53
  115.5 1.2 copy.168
  116.7 2.0 %pad_maximum_fusion = f32[13,264,136]{1,2,0:T(8,128)S(1)} fusion(f32[13,4,136]{1,2,0:T(8,128)S(1)} %copy.169, f32[13,256,4]{1,2,0:T(4,128)} %copy-done.32, f32[13,256,128]{1,2,0:T(8,128)S(1)} %constant_dynamic-update-slice_fusion, f32[13,256,4]{1,2,0:T(4,128)} %copy-done.33, f32[13,4,136]{1,2,0:T(8,128)S(1)} %copy.168), kind=kLoop, calls=%fused_computation.3 | loop fusion | flops 1867008 | bytes 3734016 | tf_op jit(solution)/shard_map/concatenate | solution.py:55
  128.6 1.7 %copy.193 = f32[256,1,3,1,256]{4,3,2,1,0:T(1,128)} copy(f32[256,1,3,1,256]{4,2,0,3,1:T(4,128)S(1)} %bitcast.362) | data formatting | bytes 1572864 | tf_op jit(solution)/shard_map/reshape | solution.py:40
  130.3 6.0 %all-to-all-start.2 = ((f32[256,1,3,1,256]{4,3,2,1,0:T(1,128)}), f32[256,1,3,1,256]{4,3,2,1,0:T(1,128)S(1)}, u32[]{:S(2)}, u32[]{:S(2)}) async-start(f32[256,1,3,1,256]{4,3,2,1,0:T(1,128)} %copy.193), calls=%async_computation.2 | async-start | bytes 1572864 | tf_op jit(solution)/shard_map/all_to_all | solution.py:41
  136.7 24.5 %all-to-all-done.2 = f32[256,1,3,1,256]{4,3,2,1,0:T(1,128)S(1)} async-done(((f32[256,1,3,1,256]{4,3,2,1,0:T(1,128)}), f32[256,1,3,1,256]{4,3,2,1,0:T(1,128)S(1)}, u32[]{:S(2)}, u32[]{:S(2)}) %all-to-all-start.2) | async-done | bytes 786464 | tf_op jit(solution)/shard_map/all_to_all | solution.py:41
  (181 shorter events, 39.8 us)
Async XLA Ops:
  0.0 19.2 %copy-start = (f32[1,7,128,256]{3,2,1,0:T(8,128)S(1)}, f32[1,7,128,256]{3,2,1,0:T(8,128)}, u32[]{:S(2)}) copy-start(f32[1,7,128,256]{3,2,1,0:T(8,128)} %param.4) | copy-start | bytes 2752516
  1.6 25.6 %all-to-all-start.1 = ((s32[256,1,1,1]{3,2,1,0:T(1,128)}), s32[256,1,1,1]{3,2,1,0:T(1,128)S(1)}, u32[]{:S(2)}, u32[]{:S(2)}) async-start(s32[256,1,1,1]{3,2,1,0:T(1,128)} %copy.145), calls=%async_computation.1 | async-start | bytes 262144 | tf_op jit(solution)/shard_map/all_to_all | solution.py:41
  22.4 13.7 %copy-start.35 = (s32[128]{0:T(128)S(1)}, s32[128]{0:T(128)}, u32[]{:S(2)}) copy-start(s32[128]{0:T(128)} %param.6) | copy-start | bytes 1540
  27.1 9.0 %copy-start.26 = (s32[256,1,1,1]{3,2,1,0:T(1,128)}, s32[256,1,1,1]{3,2,1,0:T(1,128)S(1)}, u32[]{:S(2)}) copy-start(s32[256,1,1,1]{3,2,1,0:T(1,128)S(1)} %all-to-all-done.1) | copy-start | bytes 3076
  27.1 50.6 %all-to-all-start = ((f32[256,1,6,1,256]{4,3,2,1,0:T(1,128)}), f32[256,1,6,1,256]{4,3,2,1,0:T(1,128)S(1)}, u32[]{:S(2)}, u32[]{:S(2)}) async-start(f32[256,1,6,1,256]{4,3,2,1,0:T(1,128)} %copy.141), calls=%async_computation | async-start | bytes 3145728 | tf_op jit(solution)/shard_map/all_to_all | solution.py:41
  37.0 4.7 %copy-start.3 = (f32[1,1,128,256]{3,2,1,0:T(8,128)}, f32[1,1,128,256]{3,2,1,0:T(8,128)S(1)}, u32[]{:S(2)}) copy-start(f32[1,1,128,256]{3,2,1,0:T(8,128)S(1)} %get-tuple-element.57) | copy-start | bytes 393220
  37.0 4.8 %copy-start.4 = (f32[1,1,128,256]{3,2,1,0:T(8,128)}, f32[1,1,128,256]{3,2,1,0:T(8,128)S(1)}, u32[]{:S(2)}) copy-start(f32[1,1,128,256]{3,2,1,0:T(8,128)S(1)} %get-tuple-element.58) | copy-start | bytes 393220
  43.0 5.6 %copy-start.1 = (f32[1,256,128]{1,2,0:T(8,128)S(1)}, f32[1,256,128]{1,2,0:T(8,128)}, u32[]{:S(2)}) copy-start(f32[1,256,128]{1,2,0:T(8,128)} %copy.135) | copy-start | bytes 393220
  80.6 5.8 %copy-start.2 = (f32[1,256,128]{1,2,0:T(8,128)S(1)}, f32[1,256,128]{1,2,0:T(8,128)}, u32[]{:S(2)}) copy-start(f32[1,256,128]{1,2,0:T(8,128)} %copy.135) | copy-start | bytes 393220
  87.6 3.1 %collective-permute-start.1 = (f32[13,256,4]{1,2,0:T(4,128)S(1)}, f32[13,256,4]{1,2,0:T(4,128)S(1)}, u32[]{:S(2)}, u32[]{:S(2)}) collective-permute-start(f32[13,256,4]{1,2,0:T(4,128)S(1)} %get-tuple-element.45), channel_id=1, source_target_pairs={{1,0},{2,1},{3,2},{4,3},{5,4},{6,5},{7,6},{8,7},{9,8},{10,9},{11,1... | collective-permute-start | bytes 159752 | tf_op jit(solution)/shard_map/ppermute | solution.py:54
  87.7 6.4 %collective-permute-start = (f32[13,256,4]{1,2,0:T(4,128)S(1)}, f32[13,256,4]{1,2,0:T(4,128)S(1)}, u32[]{:S(2)}, u32[]{:S(2)}) collective-permute-start(f32[13,256,4]{1,2,0:T(4,128)S(1)} %get-tuple-element.44), channel_id=1, source_target_pairs={{0,1},{1,2},{2,3},{3,4},{4,5},{5,6},{6,7},{7,8},{8,9},{9,10},{10,1... | collective-permute-start | bytes 159752 | tf_op jit(solution)/shard_map/ppermute | solution.py:53
  90.7 3.6 %copy-start.32 = (f32[13,256,4]{1,2,0:T(4,128)}, f32[13,256,4]{1,2,0:T(4,128)S(1)}, u32[]{:S(2)}) copy-start(f32[13,256,4]{1,2,0:T(4,128)S(1)} %collective-permute-done.1) | copy-start | bytes 159748
  96.1 11.5 %copy-start.25 = (f32[128,256]{1,0:T(8,128)S(1)}, f32[128,256]{1,0:T(8,128)}, u32[]{:S(2)}) copy-start(f32[128,256]{1,0:T(8,128)} %get-tuple-element.34) | copy-start | bytes 393220
  96.1 14.6 %copy-start.17 = (f32[1,128,256]{2,0,1:T(1,128)S(1)}, f32[1,128,256]{2,0,1:T(1,128)}, u32[]{:S(2)}) copy-start(f32[1,128,256]{2,0,1:T(1,128)} %copy-done.16) | copy-start | bytes 393220
  96.1 15.3 %copy-start.15 = (f32[1,128,256]{2,0,1:T(1,128)S(1)}, f32[1,128,256]{2,0,1:T(1,128)}, u32[]{:S(2)}) copy-start(f32[1,128,256]{2,0,1:T(1,128)} %copy-done.14) | copy-start | bytes 393220
  96.1 16.1 %copy-start.13 = (f32[1,128,256]{2,0,1:T(1,128)S(1)}, f32[1,128,256]{2,0,1:T(1,128)}, u32[]{:S(2)}) copy-start(f32[1,128,256]{2,0,1:T(1,128)} %copy-done.12) | copy-start | bytes 393220
  96.1 19.1 %collective-permute-start.3 = (f32[13,4,136]{2,1,0:T(4,128)}, f32[13,4,136]{2,1,0:T(4,128)S(1)}, u32[]{:S(2)}, u32[]{:S(2)}) collective-permute-start(f32[13,4,136]{2,1,0:T(4,128)} %copy.167), channel_id=1, source_target_pairs={{16,0},{32,16},{48,32},{64,48},{80,64},{96,80},{112,96},{17,1},{33... | collective-permute-start | bytes 84872 | tf_op jit(solution)/shard_map/ppermute | solution.py:54
  101.1 11.8 %copy-start.11 = (f32[1,128,256]{2,0,1:T(1,128)S(1)}, f32[1,128,256]{2,0,1:T(1,128)}, u32[]{:S(2)}) copy-start(f32[1,128,256]{2,0,1:T(1,128)} %copy-done.10) | copy-start | bytes 393220
  101.1 12.5 %copy-start.9 = (f32[1,128,256]{2,0,1:T(1,128)S(1)}, f32[1,128,256]{2,0,1:T(1,128)}, u32[]{:S(2)}) copy-start(f32[1,128,256]{2,0,1:T(1,128)} %copy-done.8) | copy-start | bytes 393220
  101.6 12.8 %copy-start.7 = (f32[1,128,256]{2,0,1:T(1,128)S(1)}, f32[1,128,256]{2,0,1:T(1,128)}, u32[]{:S(2)}) copy-start(f32[1,128,256]{2,0,1:T(1,128)} %copy-done.6) | copy-start | bytes 393220
  101.7 13.9 %collective-permute-start.2 = (f32[13,4,136]{2,1,0:T(4,128)S(1)}, f32[13,4,136]{2,1,0:T(4,128)}, u32[]{:S(2)}, u32[]{:S(2)}) collective-permute-start(f32[13,4,136]{2,1,0:T(4,128)S(1)} %copy.166), channel_id=1, source_target_pairs={{0,16},{16,32},{32,48},{48,64},{64,80},{80,96},{96,112},{1,17},{17... | collective-permute-start | bytes 84872 | tf_op jit(solution)/shard_map/ppermute | solution.py:53
  130.3 30.9 %all-to-all-start.2 = ((f32[256,1,3,1,256]{4,3,2,1,0:T(1,128)}), f32[256,1,3,1,256]{4,3,2,1,0:T(1,128)S(1)}, u32[]{:S(2)}, u32[]{:S(2)}) async-start(f32[256,1,3,1,256]{4,3,2,1,0:T(1,128)} %copy.193), calls=%async_computation.2 | async-start | bytes 1572864 | tf_op jit(solution)/shard_map/all_to_all | solution.py:41
  136.6 24.7 %copy-start.22 = (f32[1,1,128,256]{3,2,1,0:T(8,128)S(1)}, f32[1,1,128,256]{3,2,1,0:T(8,128)}, u32[]{:S(2)}) copy-start(f32[1,1,128,256]{3,2,1,0:T(8,128)} %get-tuple-element.52) | copy-start | bytes 393220
  136.7 24.7 %copy-start.23 = (f32[1,1,128,256]{3,2,1,0:T(8,128)S(1)}, f32[1,1,128,256]{3,2,1,0:T(8,128)}, u32[]{:S(2)}) copy-start(f32[1,1,128,256]{3,2,1,0:T(8,128)} %get-tuple-element.53) | copy-start | bytes 393220
  (19 other events, 29.6 us)
where the time goes:
time: 164 us; the launch traced here: 162 us
  waiting for transfers between devices  61.2 us (37%)
  local copies, waits for them, and re-layouts  43.8 us (27%)
  starting transfers between devices  39.3 us (24%)
  other arithmetic  17 us (10%)
    all_to_all x3, waiting for transfers between devices, exchange_both(): tiles = lax.all_to_all(tiles, axis, split_axis=0, concat_axis=0, tiled=True)  56.3 us
    all_to_all x3, starting transfers between devices, exchange_both(): tiles = lax.all_to_all(tiles, axis, split_axis=0, concat_axis=0, tiled=True)  29.5 us
    unnamed x83, local copies, waits for them, and re-layouts  7.29 us
    ppermute x2, starting transfers between devices, with_halo(): after = lax.ppermute(first, axis, down)  5.08 us
    ppermute x2, starting transfers between devices, with_halo(): before = lax.ppermute(last, axis, up)  4.7 us
    reshape x2, local copies, waits for them, and re-layouts, exchange_both(): tiles = tiles.reshape(-1, *inside)  4.52 us
    slice x1, local copies, waits for them, and re-layouts, prepare(): push_y = active * (concentration * forcing[1] - ice_mass * forcing[5])  4.44 us
    unnamed x6, other arithmetic  4.16 us
  transfers between devices with their start and end apart: 7, of which 5 were waited for; matrix products, arithmetic and copies ran while one was open for 19% of the time, Pallas kernels for 0%

commit v1 on v0

v1 whole, which is shorter than its diff:
```python
import functools

import jax
import jax.numpy as jnp
from jax import lax
from jax.experimental import pallas as pl
from jax.experimental.pallas import tpu as pltpu
from jax.sharding import PartitionSpec as P


NSUB = 4
NLAT = 8
NLON = 16
NT = NLAT * NLON
TOP = 16
ROWS = 160
MESH = pl.DeviceIdType.MESH
HIGHEST = lax.Precision.HIGHEST
F32 = jnp.float32

U, V, S1, S2, S12, STR, MASS, DRAG, ACT, CX, CY, PX, PY = range(13)
GROUP_ICE = (U, V, MASS, DRAG, S1, S2, S12, ACT)
GROUP_CUR = (CX, CY)
GROUP_PUSH = (PX, PY)


def lanes_of(shape):
    return lax.broadcasted_iota(jnp.int32, shape, len(shape) - 1)


def root(x):
    return x * lax.rsqrt(x)


def kernel(
    f_ref, own_ref, cov_ref, land_ref, out_ref,
    ids, sa, ra, sb, rb, x, act, gat, opn, outb, qmat,
    ss1, sn1, hs1, hn1, pk1, pw1, pe1,
    ss2, sn2, hs2, hn2, pk2, pw2, pe2,
    ss3, sn3, hs3, hn3, pk3, pw3, pe3,
    id_send, id_recv, sa_sem, ra_sem, sb_sem, rb_sem, h_send, h_recv,
):
    comp = lax.axis_index("comp")
    la = lax.axis_index("lat")
    lo = lax.axis_index("lon")
    me = la * NLON + lo
    barrier = pltpu.get_barrier_semaphore()
    sa2, ra2, sb2, rb2 = (r.reshape(4 * NT, 128) for r in (sa, ra, sb, rb))

    def target(chunk, j):
        half = lax.rem(lo // 8 + chunk // 2, 2)
        core = lax.rem(lax.rem(la, 2) + chunk % 2, 2)
        level = lax.rem(la // 2 + lax.rem(j, 4), 4)
        column = lax.rem(lax.rem(lo, 8) + j // 4, 8)
        return 2 * level + core, 8 * half + column

    def send_chunk(src, dst, send_sem, recv_sem, chunk, other):
        def body(j, carry):
            tla, tlo = target(chunk, j)
            t = tla * NLON + tlo
            pltpu.make_async_remote_copy(
                src_ref=src.at[pl.ds(4 * t, 4)],
                dst_ref=dst.at[pl.ds(4 * me, 4)],
                send_sem=send_sem,
                recv_sem=recv_sem.at[chunk],
                device_id=(other, tla, tlo),
                device_id_type=MESH,
            ).start()
            return carry

        lax.fori_loop(0, 32, body, 0)

    def wait_bytes(ref, sem):
        pltpu.make_async_copy(ref, ref, sem).wait()

    def wait_chunk(dst, recv_sem, chunk):
        wait_bytes(dst.at[pl.ds(0, 128)], recv_sem.at[chunk])

    @pl.when(comp == 0)
    def _():
        def greet(k, carry):
            t = lax.rem(me + k, NT)
            pl.semaphore_signal(barrier, inc=1, device_id=(1, t // NLON, lax.rem(t, NLON)), device_id_type=MESH)
            return carry

        lax.fori_loop(0, NT, greet, 0)
        for ch in range(2):
            for par in range(2):
                sa2[pl.ds(2 * ch + par, NT, stride=4), :] = f_ref[2 + ch, :, pl.ds(128 * par, 128)]
        pl.semaphore_wait(barrier, NT)
        for chunk in range(4):
            send_chunk(sa, ra, sa_sem, ra_sem, chunk, 1)

        def air(k, carry):
            rows = pl.ds(pl.multiple_of(8 * k, 8), 8)
            wx, wy, cx, cy, rho = (f_ref[i, rows, :] for i in (0, 1, 2, 3, 6))
            scale = rho * 0.1 * root(wx * wx + wy * wy + 1.0)
            outb[0, rows, :] = scale * wx
            outb[1, rows, :] = scale * wy
            rx = wx - cx
            ry = wy - cy
            speed = root(rx * rx + ry * ry + 1.0)
            scale = rho * (0.1 + 0.05 * speed) * speed
            opn[0, rows, :] = scale * rx
            opn[1, rows, :] = scale * ry
            return carry

        lax.fori_loop(0, 16, air, 0)

        for chunk in range(4):
            wait_chunk(ra, ra_sem, chunk)

            def push(level, carry):
                tla, tlo = target(chunk, level)
                base = tla * NLON + tlo // 8 * 8
                rows = pl.ds(pl.multiple_of(base, 8), 8)
                for par in range(2):
                    lanes = pl.ds(128 * par, 128)
                    conc = ra2[pl.ds(4 * base + par, 8, stride=4), :]
                    mass = ra2[pl.ds(4 * base + 2 + par, 8, stride=4), :]
                    for ch in range(2):
                        sb2[pl.ds(4 * base + 2 * ch + par, 8, stride=4), :] = (
                            conc * outb[ch, rows, lanes] - mass * f_ref[4 + ch, rows, lanes]
                        )
                return carry

            lax.fori_loop(0, 4, push, 0)
            send_chunk(sb, rb, sb_sem, rb_sem, chunk, 1)

        for chunk in range(4):
            wait_chunk(rb, rb_sem, chunk)
        for ch in range(2):
            for par in range(2):
                lanes = pl.ds(128 * par, 128)
                conc = ra2[pl.ds(par, NT, stride=4), :]
                out_ref[ch, :, lanes] = rb2[pl.ds(2 * ch + par, NT, stride=4), :] + (1.0 - conc) * opn[ch, :, lanes]
        wait_bytes(sa, sa_sem)
        wait_bytes(sb, sb_sem)

    east = lax.rem(lo + 1, NLON)
    west = lax.rem(lo + NLON - 1, NLON)
    has_south = la > 0
    has_north = la < NLAT - 1

    def halo_copies(group, bufs):
        ss, sn, hs, hn, pk, pw, pe = bufs
        south, north = la - 1, la + 1
        low, high = pk.at[pl.ds(0, 8)], pk.at[pl.ds(120, 8)]
        below, above = pl.ds(0, 8), pl.ds(136, 8)
        plan = (
            (None, pk, pw.at[pl.ds(8, 128)], la, east),
            (None, pk, pe.at[pl.ds(8, 128)], la, west),
            (has_north, sn, hs, north, lo),
            (has_north, high, pw.at[below], north, east),
            (has_north, high, pe.at[below], north, west),
            (has_south, ss, hn, south, lo),
            (has_south, low, pw.at[above], south, east),
            (has_south, low, pe.at[above], south, west),
        )
        return [
            (
                cond,
                pltpu.make_async_remote_copy(
                    src_ref=src, dst_ref=dst, send_sem=h_send.at[8 * group + n], recv_sem=h_recv.at[8 * group + n],
                    device_id=(1, tla, tlo), device_id_type=MESH,
                ),
            )
            for n, (cond, src, dst, tla, tlo) in enumerate(plan)
        ]

    def under(cond, action):
        if cond is None:
            action()
        else:
            pl.when(cond)(action)

    def halo_start(group, bufs, source):
        ss, sn, hs, hn, pk, pw, pe = bufs
        count = ss.shape[0]
        for n in range(count):
            ss[n] = source(n)[pl.ds(0, 8), :]
            sn[n] = source(n)[pl.ds(120, 8), :]
        lane = lanes_of((8, 128))

        def pack(k, carry):
            rows = pl.ds(pl.multiple_of(8 * k, 8), 8)
            packed = jnp.zeros((8, 128), F32)
            for n in range(count):
                for par in range(2):
                    j = 2 * n + par
                    value = source(n)[rows, pl.ds(128 * par, 128)]
                    first = value if j == 0 else pltpu.roll(value, 4 * j, 1)
                    last = pltpu.roll(value, (4 * j - 60) % 128, 1)
                    packed = jnp.where((lane >= 4 * j) & (lane < 4 * j + 4), first, packed)
                    packed = jnp.where((lane >= 64 + 4 * j) & (lane < 68 + 4 * j), last, packed)
            pk[rows, :] = packed
            return carry

        lax.fori_loop(0, 16, pack, 0)
        for cond, copy in halo_copies(group, bufs):
            under(cond, copy.start)

    def halo_walls(bufs):
        ss, sn, hs, hn, pk, pw, pe = bufs
        zero = jnp.zeros((8, 128), F32)

        @pl.when(la == 0)
        def _():
            hs[...] = jnp.zeros(hs.shape, F32)
            pw[pl.ds(0, 8), :] = zero
            pe[pl.ds(0, 8), :] = zero

        @pl.when(la == NLAT - 1)
        def _():
            hn[...] = jnp.zeros(hn.shape, F32)
            pw[pl.ds(136, 8), :] = zero
            pe[pl.ds(136, 8), :] = zero

    def halo_finish(group, bufs, channels, source):
        ss, sn, hs, hn, pk, pw, pe = bufs
        copies = halo_copies(group, bufs)
        received = {2: has_south, 3: has_south, 4: has_south, 5: has_north, 6: has_north, 7: has_north}
        for n, (cond, copy) in enumerate(copies):
            under(received.get(n), copy.wait_recv)
        for n, channel in enumerate(channels):
            for par in range(2):
                lanes = pl.ds(128 * par, 128)
                x[2 * channel + par, pl.ds(8, 8), pl.ds(0, 128)] = hs[n, :, lanes]
                x[2 * channel + par, pl.ds(144, 8), pl.ds(0, 128)] = hn[n, :, lanes]
        lane = lanes_of((8, 128))

        def unpack(k, carry):
            rows = pl.ds(pl.multiple_of(8 * k, 8), 8)
            into = pl.ds(pl.multiple_of(8 * k + 8, 8), 8)
            from_west = pw[rows, :]
            from_east = pe[rows, :]
            for n, channel in enumerate(channels):
                for par in range(2):
                    j = 2 * n + par
                    right = from_east if j == 0 else pltpu.roll(from_east, 128 - 4 * j, 1)
                    left = pltpu.roll(from_west, (60 - 4 * j) % 128, 1)
                    x[2 * channel + par, into, pl.ds(128, 128)] = jnp.where(lane < 64, right, left)
            return carry

        lax.fori_loop(0, 18, unpack, 0)

        def main(k, carry):
            rows = pl.ds(pl.multiple_of(8 * k, 8), 8)
            into = pl.ds(pl.multiple_of(8 * k + TOP, 8), 8)
            for n, channel in enumerate(channels):
                for par in range(2):
                    x[2 * channel + par, into, pl.ds(0, 128)] = source(n)[rows, pl.ds(128 * par, 128)]
            return carry

        lax.fori_loop(0, 16, main, 0)

    def halo_sent(group, bufs):
        for cond, copy in halo_copies(group, bufs):
            under(cond, copy.wait_send)

    ice_bufs = (ss1, sn1, hs1, hn1, pk1, pw1, pe1)
    cur_bufs = (ss2, sn2, hs2, hn2, pk2, pw2, pe2)
    push_bufs = (ss3, sn3, hs3, hn3, pk3, pw3, pe3)

    @pl.when(comp == 1)
    def _():
        def greet(k, carry):
            t = lax.rem(me + k, NT)
            tla, tlo = t // NLON, lax.rem(t, NLON)

            @pl.when(k > 0)
            def _():
                pl.semaphore_signal(barrier, inc=1, device_id=(1, tla, tlo), device_id_type=MESH)

            pl.semaphore_signal(barrier, inc=1, device_id=(0, tla, tlo), device_id_type=MESH)
            return carry

        lax.fori_loop(0, NT, greet, 0)

        square = (NT, NT)
        diagonal = lax.broadcasted_iota(jnp.int32, square, 0) == lanes_of(square)
        covered = jnp.sum(jnp.where(diagonal, cov_ref[...].astype(F32), 0.0), axis=1, keepdims=True)
        act[...] = covered * (1 - land_ref[...]).astype(F32)
        halo_walls(ice_bufs)
        halo_walls(cur_bufs)
        halo_walls(push_bufs)

        pl.semaphore_wait(barrier, 2 * NT - 1)

        def tell(k, carry):
            t = lax.rem(me + k, NT)
            pltpu.make_async_remote_copy(
                src_ref=own_ref, dst_ref=ids.at[me], send_sem=id_send, recv_sem=id_recv,
                device_id=(1, t // NLON, lax.rem(t, NLON)), device_id_type=MESH,
            ).start()
            return carry

        lax.fori_loop(1, NT, tell, 0)
        ids[me] = own_ref[...]

        def ice_source(n):
            return f_ref.at[n] if n < 7 else act

        halo_start(0, ice_bufs, ice_source)

        wait_bytes(ids.at[pl.ds(0, NT - 1)], id_recv)
        every = ids.reshape(NT, NT)[...]
        local = jnp.where(lanes_of(square) == me, (every - NT * me).astype(F32), 0.0)
        local = jnp.sum(local, axis=1, keepdims=True)
        q = (local == lanes_of(square).astype(F32)).astype(F32)
        qmat[0] = q
        qmat[1] = q.T

        def to_slots(values):
            return jnp.dot(qmat[0], values, precision=HIGHEST, preferred_element_type=F32)

        def to_blocks(values):
            return jnp.dot(qmat[1], values, precision=HIGHEST, preferred_element_type=F32)

        a = act[...]
        for ch, value in enumerate((f_ref[3] * a, f_ref[2] * a)):
            moved = to_slots(value)
            for par in range(2):
                sa2[pl.ds(2 * ch + par, NT, stride=4), :] = moved[:, 128 * par : 128 * par + 128]
        for chunk in range(4):
            send_chunk(sa, ra, sa_sem, ra_sem, chunk, 0)

        halo_finish(0, ice_bufs, GROUP_ICE, ice_source)

        def prepare(k, carry):
            rows = pl.ds(pl.multiple_of(8 * k + 8, 8), 8)
            for par in range(2):
                conc = x[2 * DRAG + par, rows, :]
                active = x[2 * ACT + par, rows, :]
                x[2 * STR + par, rows, :] = x[2 * MASS + par, rows, :] * jnp.exp(2.0 * (conc - 1.0)) * active
                x[2 * DRAG + par, rows, :] = 1.5 * conc * active
            return carry

        lax.fori_loop(0, 18, prepare, 0)

        for chunk in range(4):
            wait_chunk(ra, ra_sem, chunk)
        for ch in range(2):
            for par in range(2):
                gat[ch, :, pl.ds(128 * par, 128)] = to_blocks(ra2[pl.ds(2 * ch + par, NT, stride=4), :])
        halo_start(1, cur_bufs, lambda n: gat.at[n])
        halo_finish(1, cur_bufs, GROUP_CUR, lambda n: gat.at[n])

        for chunk in range(4):
            wait_chunk(rb, rb_sem, chunk)
        for ch in range(2):
            for par in range(2):
                gat[2 + ch, :, pl.ds(128 * par, 128)] = to_blocks(rb2[pl.ds(2 * ch + par, NT, stride=4), :])
        halo_start(2, push_bufs, lambda n: gat.at[2 + n])
        halo_finish(2, push_bufs, GROUP_PUSH, lambda n: gat.at[2 + n])

        def get(channel, par, start):
            return x[2 * channel + par, pl.ds(start, 8), :]

        def east_of(value):
            return pltpu.roll(value, 255, 1)

        def west_of(value):
            return pltpu.roll(value, 1, 1)

        third = 1.0 / 1.5

        sub = lax.broadcasted_iota(jnp.int32, (8, 256), 0)

        def stress(k, carry):
            r = pl.multiple_of(8 * (18 - k), 8)
            u0, u1, v0, v1 = get(U, 0, r), get(U, 1, r), get(V, 0, r), get(V, 1, r)
            rolled = (pltpu.roll(u0, 7, 0), pltpu.roll(v0, 7, 0))
            u2, v2 = (jnp.where(sub == 7, after, here) for after, here in zip(carry, rolled))
            for par, u, v, un, vn in ((0, u0, v0, u1, v1), (1, u1, v1, u2, v2)):
                sxx = east_of(u) - u
                syy = vn - v
                shear = (un - u) + (east_of(v) - v)
                div = sxx + syy
                ten = sxx - syy
                strength = get(STR, par, r)
                visc = strength * lax.rsqrt(div * div + (ten * ten + shear * shear) * 0.25 + 0.25)
                rows = pl.ds(r, 8)
                x[2 * S1 + par, rows, :] = (get(S1, par, r) + 0.5 * (visc * div - strength)) * third
                x[2 * S2 + par, rows, :] = (get(S2, par, r) + 0.125 * visc * ten) * third
                x[2 * S12 + par, rows, :] = (get(S12, par, r) + 0.0625 * visc * shear) * third
            return rolled

        def momentum(k, carry):
            r = pl.multiple_of(8 * k + 8, 8)
            even, odd = (
                (0.5 * (get(S1, p, r) + get(S2, p, r)), 0.5 * (get(S1, p, r) - get(S2, p, r)), get(S12, p, r))
                for p in (0, 1)
            )
            rolled = (pltpu.roll(odd[1], 1, 0), pltpu.roll(odd[2], 1, 0))
            before = [None] + [jnp.where(sub == 0, below, here) for below, here in zip(carry, rolled)]
            for par, here, down in ((0, even, before), (1, odd, even)):
                xx, yy, s12 = here
                force_x = xx - west_of(xx) + (s12 - down[2])
                force_y = s12 - west_of(s12) + (yy - down[1])
                u, v, cx, cy = get(U, par, r), get(V, par, r), get(CX, par, r), get(CY, par, r)
                mass = get(MASS, par, r)
                dx = cx - u
                dy = cy - v
                drag = get(DRAG, par, r) * root(dx * dx + dy * dy + 0.1)
                scale = get(ACT, par, r) / (2.0 * jnp.maximum(mass, 0.5) + drag)
                mass2 = 2.0 * mass
                turn = 0.3 * mass
                rows = pl.ds(r, 8)
                x[2 * U + par, rows, :] = scale * (mass2 * u + force_x + get(PX, par, r) + drag * cx + turn * v)
                x[2 * V + par, rows, :] = scale * (mass2 * v + force_y + get(PY, par, r) + drag * cy - turn * u)
            return rolled

        zero = jnp.zeros((8, 256), F32)
        for repeat in range(NSUB):
            lax.fori_loop(0, 18, stress, (zero, zero))
            lax.fori_loop(0, 18, momentum, (zero, zero))

        inner = pl.ds(TOP, NT)
        main = pl.ds(0, 128)
        for par in range(2):
            u, v = x[2 * U + par, inner, main], x[2 * V + par, inner, main]
            dx = u - x[2 * CX + par, inner, main]
            dy = v - x[2 * CY + par, inner, main]
            factor = x[2 * DRAG + par, inner, main] * root(dx * dx + dy * dy + 0.1)
            lanes = pl.ds(128 * par, 128)
            sb2[pl.ds(par, NT, stride=4), :] = to_slots(factor * dx)
            sb2[pl.ds(2 + par, NT, stride=4), :] = to_slots(factor * dy)
            out_ref[0, :, lanes] = u
            out_ref[1, :, lanes] = v
        for chunk in range(4):
            send_chunk(sb, rb, sb_sem, rb_sem, chunk, 0)
        wait_bytes(ids.at[pl.ds(0, NT - 1)], id_send)
        for group, bufs in enumerate((ice_bufs, cur_bufs, push_bufs)):
            halo_sent(group, bufs)
        wait_bytes(sa, sa_sem)
        wait_bytes(sb, sb_sem)


def halo_scratch(count):
    return [
        pltpu.VMEM((count, 8, 256), F32),
        pltpu.VMEM((count, 8, 256), F32),
        pltpu.VMEM((count, 8, 256), F32),
        pltpu.VMEM((count, 8, 256), F32),
        pltpu.VMEM((128, 128), F32),
        pltpu.VMEM((144, 128), F32),
        pltpu.VMEM((144, 128), F32),
    ]


def per_device(fields, block_owner, ice_covered, land_mask):
    out = pl.pallas_call(
        kernel,
        out_shape=jax.ShapeDtypeStruct((2, NT, 256), F32),
        in_specs=[pl.BlockSpec(memory_space=pltpu.VMEM)] * 4,
        out_specs=pl.BlockSpec(memory_space=pltpu.VMEM),
        scratch_shapes=[
            pltpu.VMEM((NT, 1, NT), jnp.int32),
            *[pltpu.VMEM((4 * NT, 1, 128), F32)] * 4,
            pltpu.VMEM((26, ROWS, 256), F32),
            pltpu.VMEM((NT, 256), F32),
            pltpu.VMEM((4, NT, 256), F32),
            pltpu.VMEM((2, NT, 256), F32),
            pltpu.VMEM((2, NT, 256), F32),
            pltpu.VMEM((2, NT, NT), F32),
            *halo_scratch(8),
            *halo_scratch(2),
            *halo_scratch(2),
            pltpu.SemaphoreType.DMA,
            pltpu.SemaphoreType.DMA,
            pltpu.SemaphoreType.DMA,
            pltpu.SemaphoreType.DMA((4,)),
            pltpu.SemaphoreType.DMA,
            pltpu.SemaphoreType.DMA((4,)),
            pltpu.SemaphoreType.DMA((24,)),
            pltpu.SemaphoreType.DMA((24,)),
        ],
        compiler_params=pltpu.CompilerParams(
            collective_id=0, has_side_effects=True, vmem_limit_bytes=40 * 1024 * 1024
        ),
    )(fields[0], block_owner.reshape(1, NT), ice_covered.reshape(1, NT), land_mask)
    return out[None]


def solution(mesh):
    placed = (
        P("comp", None, ("lat", "lon"), None),
        P(("lat", "lon")),
        P(("lat", "lon")),
        P(("lat", "lon"), None),
    )
    return jax.shard_map(
        per_device,
        mesh=mesh,
        in_specs=placed,
        out_specs=P("comp", None, ("lat", "lon"), None),
        check_vma=False,
    )
```

time: 164 us -> 91.8 us (0.56)
  Pallas kernels: 0 us -> 86.5 us
  waiting for transfers between devices: 61.2 us -> 0 us
  local copies, waits for them, and re-layouts: 43.8 us -> 3.46 us
  starting transfers between devices: 39.3 us -> 0 us
  other arithmetic: 17 us -> 0 us
    pallas_call x0 -> x1, Pallas kernels: none -> 86.5 us  [per_device(): pl.pallas_call(kernel, out_shape=jax.ShapeDtypeStruct((2, NT, 256), F32),...]
    all_to_all x3 -> x0, waiting for transfers between devices: 56.3 us -> none  [exchange_both(): tiles = lax.all_to_all(tiles, axis, split_axis=0, concat_axis=0, tiled=True)]
    all_to_all x3 -> x0, starting transfers between devices: 29.5 us -> none  [exchange_both(): tiles = lax.all_to_all(tiles, axis, split_axis=0, concat_axis=0, tiled=True)]
    slice x17 -> x0, local copies, waits for them, and re-layouts: 10.4 us -> none  [the longest x1 4.44 us: prepare(): push_y = active * (concentration * forcing[1] - ice_mass * forcing[5])]
    ppermute x4 -> x0, starting transfers between devices: 9.77 us -> none  [the longest x2 5.08 us: with_halo(): after = lax.ppermute(first, axis, down)]
    squeeze x18 -> x0, local copies, waits for them, and re-layouts: 7.01 us -> none  [the longest x4 2.42 us: prepare(): concentration = ice_tile[3]]
    reshape x5 -> x0, local copies, waits for them, and re-layouts: 6.52 us -> none  [the longest x2 4.52 us: exchange_both(): tiles = tiles.reshape(-1, *inside)]
    another operation x14 -> x0, local copies, waits for them, and re-layouts: 6.09 us -> none  [the longest x4 3.17 us: subcycle(): strength, ice_mass, drag_base, push_x, push_y, current_x, current_y, acti...]
  transfers between devices with their start and end apart: 7 -> 0, of which waited for: 5 -> 0; matrix products, arithmetic and copies ran while one was open for 19% -> 0% of each run, Pallas kernels for 0% -> 0%
where the time goes in v1:
time: 91.8 us; the launch traced here: 90 us
  Pallas kernels  86.5 us (94%)
  local copies, waits for them, and re-layouts  3.46 us (4%)
    pallas_call x1, Pallas kernels, per_device(): pl.pallas_call(kernel, out_shape=jax.ShapeDtypeStruct((2, NT, 256), F32),...  86.5 us
    unnamed x9, local copies, waits for them, and re-layouts  3.46 us

profile of v1, /device:TPU:65, one launch (start us, length us, event | category | flops | bytes accessed | tf_op | source)
XLA Modules:
  0.0 90.0 jit_solution(14121451597781143992)
XLA Ops:
  0.0 0.0 copy-start.2
  0.0 0.0 copy-start.3
  0.0 0.7 copy-done.2
  0.7 0.0 copy-done.3
  0.7 0.0 copy-start
  0.7 1.2 %copy-done = f32[1,7,128,256]{3,2,1,0:T(8,128)S(1)} copy-done((f32[1,7,128,256]{3,2,1,0:T(8,128)S(1)}, f32[1,7,128,256]{3,2,1,0:T(8,128)}, u32[]{:S(2)}) %copy-start) | copy-done | bytes 917528
  1.9 0.0 copy-start.1
  1.9 0.9 %copy-done.1 = s32[128,256]{1,0:T(8,128)S(1)} copy-done((s32[128,256]{1,0:T(8,128)S(1)}, s32[128,256]{1,0:T(8,128)}, u32[]{:S(2)}) %copy-start.1) | copy-done | bytes 131096
  2.8 86.5 %shard_map.46 = f32[2,128,256]{2,1,0:T(8,128)S(1)} custom-call(f32[7,128,256]{2,1,0:T(8,128)S(1)} %bitcast.5, s32[1,128]{1,0:T(1,128)S(1)} %bitcast.6, s32[1,128]{1,0:T(1,128)S(1)} %bitcast.7, s32[128,256]{1,0:T(8,128)S(1)} %copy-done.1), custom_call_target="tpu_custom_call" | custom-call | tf_op jit(solution)/shard_map/pallas_call | solution.py:453
  89.3 0.7 copy.6
Async XLA Ops:
  0.0 0.7 copy-start.2
  0.0 0.7 copy-start.3
  0.7 1.2 %copy-start = (f32[1,7,128,256]{3,2,1,0:T(8,128)S(1)}, f32[1,7,128,256]{3,2,1,0:T(8,128)}, u32[]{:S(2)}) copy-start(f32[1,7,128,256]{3,2,1,0:T(8,128)} %param.4) | copy-start | bytes 2752516
  1.9 0.9 %copy-start.1 = (s32[128,256]{1,0:T(8,128)S(1)}, s32[128,256]{1,0:T(8,128)}, u32[]{:S(2)}) copy-start(s32[128,256]{1,0:T(8,128)} %land_ref.1) | copy-start | bytes 393220

commit v2 on v1

--- a/solution.py
+++ b/solution.py
@@ -18,7 +18,8 @@
 HIGHEST = lax.Precision.HIGHEST
 F32 = jnp.float32
 
-U, V, S1, S2, S12, STR, MASS, DRAG, ACT, CX, CY, PX, PY = range(13)
+U, V, S1, S2, S12, STR, MASS, DRAG, ACT, CX, CY, PX, PY, SCALE = range(14)
+RB = 16
 GROUP_ICE = (U, V, MASS, DRAG, S1, S2, S12, ACT)
 GROUP_CUR = (CX, CY)
 GROUP_PUSH = (PX, PY)
@@ -33,7 +34,8 @@
 
 
 def kernel(
-    f_ref, own_ref, cov_ref, land_ref, out_ref,
+    f_hbm, own_hbm, cov_hbm, land_hbm, out_ref,
+    f_ref, own_ref, cov_ref, land_ref, in_sem,
     ids, sa, ra, sb, rb, x, act, gat, opn, outb, qmat,
     ss1, sn1, hs1, hn1, pk1, pw1, pe1,
     ss2, sn2, hs2, hn2, pk2, pw2, pe2,
@@ -47,28 +49,46 @@
     barrier = pltpu.get_barrier_semaphore()
     sa2, ra2, sb2, rb2 = (r.reshape(4 * NT, 128) for r in (sa, ra, sb, rb))
 
-    def target(chunk, j):
-        half = lax.rem(lo // 8 + chunk // 2, 2)
+    loads = [
+        pltpu.make_async_copy(src, dst, in_sem.at[n])
+        for n, (src, dst) in enumerate(
+            ((f_hbm, f_ref), (own_hbm, own_ref), (cov_hbm, cov_ref), (land_hbm, land_ref))
+        )
+    ]
+
+    def greet(other):
+        for tla in range(NLAT):
+            for tlo in range(NLON):
+                pl.semaphore_signal(barrier, inc=1, device_id=(other, tla, tlo), device_id_type=MESH)
+
+    def target_core(chunk, level):
         core = lax.rem(lax.rem(la, 2) + chunk % 2, 2)
-        level = lax.rem(la // 2 + lax.rem(j, 4), 4)
-        column = lax.rem(lax.rem(lo, 8) + j // 4, 8)
-        return 2 * level + core, 8 * half + column
+        return 2 * lax.rem(la // 2 + level, 4) + core
+
+    def target_half(chunk):
+        return 8 * lax.rem(lo // 8 + chunk // 2, 2)
+
+    columns = [lax.rem(lax.rem(lo, 8) + j, 8) for j in range(8)]
+    mine = pl.ds(4 * me, 4)
 
     def send_chunk(src, dst, send_sem, recv_sem, chunk, other):
-        def body(j, carry):
-            tla, tlo = target(chunk, j)
-            t = tla * NLON + tlo
-            pltpu.make_async_remote_copy(
-                src_ref=src.at[pl.ds(4 * t, 4)],
-                dst_ref=dst.at[pl.ds(4 * me, 4)],
-                send_sem=send_sem,
-                recv_sem=recv_sem.at[chunk],
-                device_id=(other, tla, tlo),
-                device_id_type=MESH,
-            ).start()
+        half = target_half(chunk)
+
+        def body(level, carry):
+            tla = target_core(chunk, level)
+            base = tla * NLON + half
+            for column in columns:
+                pltpu.make_async_remote_copy(
+                    src_ref=src.at[pl.ds(4 * (base + column), 4)],
+                    dst_ref=dst.at[mine],
+                    send_sem=send_sem,
+                    recv_sem=recv_sem.at[chunk],
+                    device_id=(other, tla, half + column),
+                    device_id_type=MESH,
+                ).start()
             return carry
 
-        lax.fori_loop(0, 32, body, 0)
+        lax.fori_loop(0, 4, body, 0)
 
     def wait_bytes(ref, sem):
         pltpu.make_async_copy(ref, ref, sem).wait()
@@ -78,12 +98,9 @@
 
     @pl.when(comp == 0)
     def _():
-        def greet(k, carry):
-            t = lax.rem(me + k, NT)
-            pl.semaphore_signal(barrier, inc=1, device_id=(1, t // NLON, lax.rem(t, NLON)), device_id_type=MESH)
-            return carry
-
-        lax.fori_loop(0, NT, greet, 0)
+        loads[0].start()
+        greet(1)
+        loads[0].wait()
         for ch in range(2):
             for par in range(2):
                 sa2[pl.ds(2 * ch + par, NT, stride=4), :] = f_ref[2 + ch, :, pl.ds(128 * par, 128)]
@@ -111,8 +128,7 @@
             wait_chunk(ra, ra_sem, chunk)
 
             def push(level, carry):
-                tla, tlo = target(chunk, level)
-                base = tla * NLON + tlo // 8 * 8
+                base = target_core(chunk, level) * NLON + target_half(chunk)
                 rows = pl.ds(pl.multiple_of(base, 8), 8)
                 for par in range(2):
                     lanes = pl.ds(128 * par, 128)
@@ -180,23 +196,17 @@
         for n in range(count):
             ss[n] = source(n)[pl.ds(0, 8), :]
             sn[n] = source(n)[pl.ds(120, 8), :]
-        lane = lanes_of((8, 128))
-
-        def pack(k, carry):
-            rows = pl.ds(pl.multiple_of(8 * k, 8), 8)
-            packed = jnp.zeros((8, 128), F32)
-            for n in range(count):
-                for par in range(2):
-                    j = 2 * n + par
-                    value = source(n)[rows, pl.ds(128 * par, 128)]
-                    first = value if j == 0 else pltpu.roll(value, 4 * j, 1)
-                    last = pltpu.roll(value, (4 * j - 60) % 128, 1)
-                    packed = jnp.where((lane >= 4 * j) & (lane < 4 * j + 4), first, packed)
-                    packed = jnp.where((lane >= 64 + 4 * j) & (lane < 68 + 4 * j), last, packed)
-            pk[rows, :] = packed
-            return carry
-
-        lax.fori_loop(0, 16, pack, 0)
+        lane = lanes_of((NT, 128))
+        packed = jnp.zeros((NT, 128), F32)
+        for n in range(count):
+            for par in range(2):
+                j = 2 * n + par
+                value = source(n)[:, pl.ds(128 * par, 128)]
+                first = value if j == 0 else pltpu.roll(value, 4 * j, 1)
+                last = pltpu.roll(value, (4 * j - 60) % 128, 1)
+                packed = jnp.where((lane >= 4 * j) & (lane < 4 * j + 4), first, packed)
+                packed = jnp.where((lane >= 64 + 4 * j) & (lane < 68 + 4 * j), last, packed)
+        pk[...] = packed
         for cond, copy in halo_copies(group, bufs):
             under(cond, copy.start)
 
@@ -216,43 +226,33 @@
             pw[pl.ds(136, 8), :] = zero
             pe[pl.ds(136, 8), :] = zero
 
-    def halo_finish(group, bufs, channels, source):
+    def halo_finish(group, bufs, channels, source, put):
         ss, sn, hs, hn, pk, pw, pe = bufs
         copies = halo_copies(group, bufs)
         received = {2: has_south, 3: has_south, 4: has_south, 5: has_north, 6: has_north, 7: has_north}
         for n, (cond, copy) in enumerate(copies):
             under(received.get(n), copy.wait_recv)
+        lane = lanes_of((144, 128))
+        from_west = pw[...]
+        from_east = pe[...]
         for n, channel in enumerate(channels):
             for par in range(2):
+                j = 2 * n + par
                 lanes = pl.ds(128 * par, 128)
-                x[2 * channel + par, pl.ds(8, 8), pl.ds(0, 128)] = hs[n, :, lanes]
-                x[2 * channel + par, pl.ds(144, 8), pl.ds(0, 128)] = hn[n, :, lanes]
-        lane = lanes_of((8, 128))
-
-        def unpack(k, carry):
-            rows = pl.ds(pl.multiple_of(8 * k, 8), 8)
-            into = pl.ds(pl.multiple_of(8 * k + 8, 8), 8)
-            from_west = pw[rows, :]
-            from_east = pe[rows, :]
-            for n, channel in enumerate(channels):
-                for par in range(2):
-                    j = 2 * n + par
-                    right = from_east if j == 0 else pltpu.roll(from_east, 128 - 4 * j, 1)
-                    left = pltpu.roll(from_west, (60 - 4 * j) % 128, 1)
-                    x[2 * channel + par, into, pl.ds(128, 128)] = jnp.where(lane < 64, right, left)
-            return carry
-
-        lax.fori_loop(0, 18, unpack, 0)
-
-        def main(k, carry):
-            rows = pl.ds(pl.multiple_of(8 * k, 8), 8)
-            into = pl.ds(pl.multiple_of(8 * k + TOP, 8), 8)
-            for n, channel in enumerate(channels):
-                for par in range(2):
-                    x[2 * channel + par, into, pl.ds(0, 128)] = source(n)[rows, pl.ds(128 * par, 128)]
-            return carry
-
-        lax.fori_loop(0, 16, main, 0)
+                right = from_east if j == 0 else pltpu.roll(from_east, 128 - 4 * j, 1)
+                left = pltpu.roll(from_west, (60 - 4 * j) % 128, 1)
+                put(channel, par, pl.ds(8, 144), pl.ds(128, 128), jnp.where(lane < 64, right, left))
+                put(channel, par, pl.ds(8, 8), pl.ds(0, 128), hs[n, :, lanes])
+                put(channel, par, pl.ds(144, 8), pl.ds(0, 128), hn[n, :, lanes])
+                put(channel, par, pl.ds(TOP, NT), pl.ds(0, 128), source(n)[:, lanes])
+
+    def put_x(channel, par, rows, lanes, value):
+        x[2 * channel + par, rows, lanes] = value
+
+    def put_push(channel, par, rows, lanes, value):
+        put_x(channel, par, rows, lanes, value)
+        velocity = 2 * (U if channel == PX else V) + par
+        x[velocity, rows, lanes] += x[2 * SCALE + par, rows, lanes] * value
 
     def halo_sent(group, bufs):
         for cond, copy in halo_copies(group, bufs):
@@ -264,19 +264,12 @@
 
     @pl.when(comp == 1)
     def _():
-        def greet(k, carry):
-            t = lax.rem(me + k, NT)
-            tla, tlo = t // NLON, lax.rem(t, NLON)
-
-            @pl.when(k > 0)
-            def _():
-                pl.semaphore_signal(barrier, inc=1, device_id=(1, tla, tlo), device_id_type=MESH)
-
-            pl.semaphore_signal(barrier, inc=1, device_id=(0, tla, tlo), device_id_type=MESH)
-            return carry
-
-        lax.fori_loop(0, NT, greet, 0)
-
+        for load in loads:
+            load.start()
+        greet(0)
+        greet(1)
+        for load in loads:
+            load.wait()
         square = (NT, NT)
         diagonal = lax.broadcasted_iota(jnp.int32, square, 0) == lanes_of(square)
         covered = jnp.sum(jnp.where(diagonal, cov_ref[...].astype(F32), 0.0), axis=1, keepdims=True)
@@ -285,17 +278,26 @@
         halo_walls(cur_bufs)
         halo_walls(push_bufs)
 
-        pl.semaphore_wait(barrier, 2 * NT - 1)
-
-        def tell(k, carry):
-            t = lax.rem(me + k, NT)
+        pl.semaphore_wait(barrier, 2 * NT)
+
+        others = [lax.rem(lo + j, NLON) for j in range(NLON)]
+
+        def tell_one(tla, tlo):
             pltpu.make_async_remote_copy(
                 src_ref=own_ref, dst_ref=ids.at[me], send_sem=id_send, recv_sem=id_recv,
-                device_id=(1, t // NLON, lax.rem(t, NLON)), device_id_type=MESH,
+                device_id=(1, tla, tlo), device_id_type=MESH,
             ).start()
+
+        for tlo in others[1:]:
+            tell_one(la, tlo)
+
+        def tell(k, carry):
+            tla = lax.rem(la + k, NLAT)
+            for tlo in others:
+                tell_one(tla, tlo)
             return carry
 
-        lax.fori_loop(1, NT, tell, 0)
+        lax.fori_loop(1, NLAT, tell, 0)
         ids[me] = own_ref[...]
 
         def ice_source(n):
@@ -325,7 +327,7 @@
         for chunk in range(4):
             send_chunk(sa, ra, sa_sem, ra_sem, chunk, 0)
 
-        halo_finish(0, ice_bufs, GROUP_ICE, ice_source)
+        halo_finish(0, ice_bufs, GROUP_ICE, ice_source, put_x)
 
         def prepare(k, carry):
             rows = pl.ds(pl.multiple_of(8 * k + 8, 8), 8)
@@ -344,18 +346,10 @@
             for par in range(2):
                 gat[ch, :, pl.ds(128 * par, 128)] = to_blocks(ra2[pl.ds(2 * ch + par, NT, stride=4), :])
         halo_start(1, cur_bufs, lambda n: gat.at[n])
-        halo_finish(1, cur_bufs, GROUP_CUR, lambda n: gat.at[n])
-
-        for chunk in range(4):
-            wait_chunk(rb, rb_sem, chunk)
-        for ch in range(2):
-            for par in range(2):
-                gat[2 + ch, :, pl.ds(128 * par, 128)] = to_blocks(rb2[pl.ds(2 * ch + par, NT, stride=4), :])
-        halo_start(2, push_bufs, lambda n: gat.at[2 + n])
-        halo_finish(2, push_bufs, GROUP_PUSH, lambda n: gat.at[2 + n])
+        halo_finish(1, cur_bufs, GROUP_CUR, lambda n: gat.at[n], put_x)
 
         def get(channel, par, start):
-            return x[2 * channel + par, pl.ds(start, 8), :]
+            return x[2 * channel + par, pl.ds(start, RB), :]
 
         def east_of(value):
             return pltpu.roll(value, 255, 1)
@@ -364,14 +358,15 @@
             return pltpu.roll(value, 1, 1)
 
         third = 1.0 / 1.5
-
-        sub = lax.broadcasted_iota(jnp.int32, (8, 256), 0)
+        sub = lax.broadcasted_iota(jnp.int32, (RB, 256), 0)
+        zero = jnp.zeros((RB, 256), F32)
+        steps = 144 // RB
 
         def stress(k, carry):
-            r = pl.multiple_of(8 * (18 - k), 8)
+            r = pl.multiple_of(RB * (steps - 1 - k) + 8, 8)
             u0, u1, v0, v1 = get(U, 0, r), get(U, 1, r), get(V, 0, r), get(V, 1, r)
-            rolled = (pltpu.roll(u0, 7, 0), pltpu.roll(v0, 7, 0))
-            u2, v2 = (jnp.where(sub == 7, after, here) for after, here in zip(carry, rolled))
+            rolled = (pltpu.roll(u0, RB - 1, 0), pltpu.roll(v0, RB - 1, 0))
+            u2, v2 = (jnp.where(sub == RB - 1, after, here) for after, here in zip(carry, rolled))
             for par, u, v, un, vn in ((0, u0, v0, u1, v1), (1, u1, v1, u2, v2)):
                 sxx = east_of(u) - u
                 syy = vn - v
@@ -380,14 +375,14 @@
                 ten = sxx - syy
                 strength = get(STR, par, r)
                 visc = strength * lax.rsqrt(div * div + (ten * ten + shear * shear) * 0.25 + 0.25)
-                rows = pl.ds(r, 8)
+                rows = pl.ds(r, RB)
                 x[2 * S1 + par, rows, :] = (get(S1, par, r) + 0.5 * (visc * div - strength)) * third
                 x[2 * S2 + par, rows, :] = (get(S2, par, r) + 0.125 * visc * ten) * third
                 x[2 * S12 + par, rows, :] = (get(S12, par, r) + 0.0625 * visc * shear) * third
             return rolled
 
-        def momentum(k, carry):
-            r = pl.multiple_of(8 * k + 8, 8)
+        def momentum(first, k, carry):
+            r = pl.multiple_of(RB * k + 8, 8)
             even, odd = (
                 (0.5 * (get(S1, p, r) + get(S2, p, r)), 0.5 * (get(S1, p, r) - get(S2, p, r)), get(S12, p, r))
                 for p in (0, 1)
@@ -406,15 +401,32 @@
                 scale = get(ACT, par, r) / (2.0 * jnp.maximum(mass, 0.5) + drag)
                 mass2 = 2.0 * mass
                 turn = 0.3 * mass
-                rows = pl.ds(r, 8)
-                x[2 * U + par, rows, :] = scale * (mass2 * u + force_x + get(PX, par, r) + drag * cx + turn * v)
-                x[2 * V + par, rows, :] = scale * (mass2 * v + force_y + get(PY, par, r) + drag * cy - turn * u)
+                rows = pl.ds(r, RB)
+                if first:
+                    x[2 * SCALE + par, rows, :] = scale
+                else:
+                    force_x = force_x + get(PX, par, r)
+                    force_y = force_y + get(PY, par, r)
+                x[2 * U + par, rows, :] = scale * (mass2 * u + force_x + drag * cx + turn * v)
+                x[2 * V + par, rows, :] = scale * (mass2 * v + force_y + drag * cy - turn * u)
             return rolled
 
-        zero = jnp.zeros((8, 256), F32)
-        for repeat in range(NSUB):
-            lax.fori_loop(0, 18, stress, (zero, zero))
-            lax.fori_loop(0, 18, momentum, (zero, zero))
+        def subcycle(first):
+            lax.fori_loop(0, steps, stress, (zero, zero))
+            lax.fori_loop(0, steps, functools.partial(momentum, first), (zero, zero))
+
+        subcycle(True)
+
+        for chunk in range(4):
+            wait_chunk(rb, rb_sem, chunk)
+        for ch in range(2):
+            for par in range(2):
+                gat[2 + ch, :, pl.ds(128 * par, 128)] = to_blocks(rb2[pl.ds(2 * ch + par, NT, stride=4), :])
+        halo_start(2, push_bufs, lambda n: gat.at[2 + n])
+        halo_finish(2, push_bufs, GROUP_PUSH, lambda n: gat.at[2 + n], put_push)
+
+        for repeat in range(NSUB - 1):
+            subcycle(False)
 
         inner = pl.ds(TOP, NT)
         main = pl.ds(0, 128)
@@ -453,12 +465,17 @@
     out = pl.pallas_call(
         kernel,
         out_shape=jax.ShapeDtypeStruct((2, NT, 256), F32),
-        in_specs=[pl.BlockSpec(memory_space=pltpu.VMEM)] * 4,
+        in_specs=[pl.BlockSpec(memory_space=pltpu.HBM)] * 4,
         out_specs=pl.BlockSpec(memory_space=pltpu.VMEM),
         scratch_shapes=[
+            pltpu.VMEM((7, NT, 256), F32),
+            pltpu.VMEM((1, NT), jnp.int32),
+            pltpu.VMEM((1, NT), jnp.int32),
+            pltpu.VMEM((NT, 256), jnp.int32),
+            pltpu.SemaphoreType.DMA((4,)),
             pltpu.VMEM((NT, 1, NT), jnp.int32),
             *[pltpu.VMEM((4 * NT, 1, 128), F32)] * 4,
-            pltpu.VMEM((26, ROWS, 256), F32),
+            pltpu.VMEM((28, ROWS, 256), F32),
             pltpu.VMEM((NT, 256), F32),
             pltpu.VMEM((4, NT, 256), F32),
             pltpu.VMEM((2, NT, 256), F32),
@@ -477,7 +494,7 @@
             pltpu.SemaphoreType.DMA((24,)),
         ],
         compiler_params=pltpu.CompilerParams(
-            collective_id=0, has_side_effects=True, vmem_limit_bytes=40 * 1024 * 1024
+            collective_id=0, has_side_effects=True, vmem_limit_bytes=60 * 1024 * 1024
         ),
     )(fields[0], block_owner.reshape(1, NT), ice_covered.reshape(1, NT), land_mask)
     return out[None]

time: 91.8 us -> 76.8 us (0.84)
  Pallas kernels: 86.5 us -> 73.6 us
  local copies, waits for them, and re-layouts: 3.46 us -> 1.67 us
    pallas_call x1, Pallas kernels: 86.5 us -> 73.6 us  [per_device(): pl.pallas_call(kernel, out_shape=jax.ShapeDtypeStruct((2, NT, 256), F32),...]
    unnamed x9 -> x1, local copies, waits for them, and re-layouts: 3.46 us -> 1.67 us
where the time goes in v2:
time: 76.8 us; the launch traced here: 75.3 us
  Pallas kernels  73.6 us (96%)
  local copies, waits for them, and re-layouts  1.67 us (2%)
    pallas_call x1, Pallas kernels, per_device(): pl.pallas_call(kernel, out_shape=jax.ShapeDtypeStruct((2, NT, 256), F32),...  73.6 us
    unnamed x1, local copies, waits for them, and re-layouts  1.67 us

profile of v2, /device:TPU:65, one launch (start us, length us, event | category | flops | bytes accessed | tf_op | source)
XLA Modules:
  0.0 75.3 jit_solution(7842995098927292841)
XLA Ops:
  0.0 73.6 %shard_map.46 = f32[2,128,256]{2,1,0:T(8,128)} custom-call(f32[7,128,256]{2,1,0:T(8,128)} %bitcast.5, s32[1,128]{1,0:T(1,128)} %bitcast.6, s32[1,128]{1,0:T(1,128)} %bitcast.7, s32[128,256]{1,0:T(8,128)} %land_hbm.1), custom_call_target="tpu_custom_call" | custom-call | tf_op jit(solution)/shard_map/pallas_call | solution.py:465
  73.6 1.7 %copy.6 = f32[1,2,128,256]{3,2,1,0:T(8,128)} copy(f32[1,2,128,256]{3,2,1,0:T(8,128)} %bitcast.4) | data formatting | bytes 524288

commit v3 on v2

--- a/solution.py
+++ b/solution.py
@@ -36,11 +36,11 @@
 def kernel(
     f_hbm, own_hbm, cov_hbm, land_hbm, out_ref,
     f_ref, own_ref, cov_ref, land_ref, in_sem,
-    ids, sa, ra, sb, rb, x, act, gat, opn, outb, qmat,
-    ss1, sn1, hs1, hn1, pk1, pw1, pe1,
-    ss2, sn2, hs2, hn2, pk2, pw2, pe2,
-    ss3, sn3, hs3, hn3, pk3, pw3, pe3,
-    id_send, id_recv, sa_sem, ra_sem, sb_sem, rb_sem, h_send, h_recv,
+    ids, sa, ra, sb, rb, sd, rd, x, act, gat, opn, outb, qmat,
+    ss1, sn1, hs1, hn1, se1, sw1, pw1, pe1,
+    ss2, sn2, hs2, hn2, se2, sw2, pw2, pe2,
+    ss3, sn3, hs3, hn3, se3, sw3, pw3, pe3,
+    id_send, id_recv, sa_sem, ra_sem, sb_sem, rb_sem, sd_sem, rd_sem, h_send, h_recv,
 ):
     comp = lax.axis_index("comp")
     la = lax.axis_index("lat")
@@ -48,6 +48,7 @@
     me = la * NLON + lo
     barrier = pltpu.get_barrier_semaphore()
     sa2, ra2, sb2, rb2 = (r.reshape(4 * NT, 128) for r in (sa, ra, sb, rb))
+    sd2, rd2 = (r.reshape(8 * NT, 128) for r in (sd, rd))
 
     loads = [
         pltpu.make_async_copy(src, dst, in_sem.at[n])
@@ -61,40 +62,36 @@
             for tlo in range(NLON):
                 pl.semaphore_signal(barrier, inc=1, device_id=(other, tla, tlo), device_id_type=MESH)
 
-    def target_core(chunk, level):
-        core = lax.rem(lax.rem(la, 2) + chunk % 2, 2)
-        return 2 * lax.rem(la // 2 + level, 4) + core
-
-    def target_half(chunk):
-        return 8 * lax.rem(lo // 8 + chunk // 2, 2)
-
-    columns = [lax.rem(lax.rem(lo, 8) + j, 8) for j in range(8)]
-    mine = pl.ds(4 * me, 4)
-
-    def send_chunk(src, dst, send_sem, recv_sem, chunk, other):
-        half = target_half(chunk)
-
-        def body(level, carry):
-            tla = target_core(chunk, level)
-            base = tla * NLON + half
-            for column in columns:
+    others = [lax.rem(lo + j, NLON) for j in range(NLON)]
+
+    def target_lat(chunk, k, other):
+        offset = 2 * chunk + k
+        return lax.rem(la + (NLAT - offset if other == 1 else offset), NLAT)
+
+    def send_chunk(src, dst, send_sem, recv_sem, chunk, other, stride=4, rows=4):
+        def body(k, carry):
+            tla = target_lat(chunk, k, other)
+            for tlo in others:
                 pltpu.make_async_remote_copy(
-                    src_ref=src.at[pl.ds(4 * (base + column), 4)],
-                    dst_ref=dst.at[mine],
+                    src_ref=src.at[pl.ds(stride * (tla * NLON + tlo), rows)],
+                    dst_ref=dst.at[pl.ds(stride * me, rows)],
                     send_sem=send_sem,
                     recv_sem=recv_sem.at[chunk],
-                    device_id=(other, tla, half + column),
+                    device_id=(other, tla, tlo),
                     device_id_type=MESH,
                 ).start()
             return carry
 
-        lax.fori_loop(0, 4, body, 0)
+        lax.fori_loop(0, 2, body, 0)
 
     def wait_bytes(ref, sem):
         pltpu.make_async_copy(ref, ref, sem).wait()
 
-    def wait_chunk(dst, recv_sem, chunk):
-        wait_bytes(dst.at[pl.ds(0, 128)], recv_sem.at[chunk])
+    def wait_chunk(dst, recv_sem, chunk, rows=4):
+        wait_bytes(dst.at[pl.ds(0, 32 * rows)], recv_sem.at[chunk])
+
+    def rows_of(chunk, level):
+        return pl.multiple_of(target_lat(chunk, level // 2, 1) * NLON + 8 * lax.rem(level, 2), 8)
 
     @pl.when(comp == 0)
     def _():
@@ -104,10 +101,6 @@
         for ch in range(2):
             for par in range(2):
                 sa2[pl.ds(2 * ch + par, NT, stride=4), :] = f_ref[2 + ch, :, pl.ds(128 * par, 128)]
-        pl.semaphore_wait(barrier, NT)
-        for chunk in range(4):
-            send_chunk(sa, ra, sa_sem, ra_sem, chunk, 1)
-
         def air(k, carry):
             rows = pl.ds(pl.multiple_of(8 * k, 8), 8)
             wx, wy, cx, cy, rho = (f_ref[i, rows, :] for i in (0, 1, 2, 3, 6))
@@ -124,12 +117,28 @@
 
         lax.fori_loop(0, 16, air, 0)
 
+
+        def direct(level, carry):
+            base = rows_of(0, level)
+            for par in range(2):
+                lanes = pl.ds(128 * par, 128)
+                for ch in range(2):
+                    sd2[pl.ds(8 * base + 2 * ch + par, 8, stride=8), :] = outb[ch, pl.ds(base, 8), lanes]
+                    sd2[pl.ds(8 * base + 4 + 2 * ch + par, 8, stride=8), :] = f_ref[4 + ch, pl.ds(base, 8), lanes]
+            return carry
+
+        lax.fori_loop(0, 4, direct, 0)
+        pl.semaphore_wait(barrier, NT)
         for chunk in range(4):
+            send_chunk(sa, ra, sa_sem, ra_sem, chunk, 1)
+        send_chunk(sd, rd, sd_sem, rd_sem, 0, 1, 8, 8)
+
+        for chunk in range(1, 4):
             wait_chunk(ra, ra_sem, chunk)
 
             def push(level, carry):
-                base = target_core(chunk, level) * NLON + target_half(chunk)
-                rows = pl.ds(pl.multiple_of(base, 8), 8)
+                base = rows_of(chunk, level)
+                rows = pl.ds(base, 8)
                 for par in range(2):
                     lanes = pl.ds(128 * par, 128)
                     conc = ra2[pl.ds(4 * base + par, 8, stride=4), :]
@@ -145,13 +154,15 @@
 
         for chunk in range(4):
             wait_chunk(rb, rb_sem, chunk)
+        wait_chunk(ra, ra_sem, 0, 2)
         for ch in range(2):
             for par in range(2):
                 lanes = pl.ds(128 * par, 128)
                 conc = ra2[pl.ds(par, NT, stride=4), :]
                 out_ref[ch, :, lanes] = rb2[pl.ds(2 * ch + par, NT, stride=4), :] + (1.0 - conc) * opn[ch, :, lanes]
         wait_bytes(sa, sa_sem)
-        wait_bytes(sb, sb_sem)
+        wait_bytes(sb.at[pl.ds(0, 384)], sb_sem)
+        wait_bytes(sd.at[pl.ds(0, 256)], sd_sem)
 
     east = lax.rem(lo + 1, NLON)
     west = lax.rem(lo + NLON - 1, NLON)
@@ -159,19 +170,20 @@
     has_north = la < NLAT - 1
 
     def halo_copies(group, bufs):
-        ss, sn, hs, hn, pk, pw, pe = bufs
+        ss, sn, hs, hn, se, sw, pw, pe = bufs
+        size = se.shape[0]
         south, north = la - 1, la + 1
-        low, high = pk.at[pl.ds(0, 8)], pk.at[pl.ds(120, 8)]
-        below, above = pl.ds(0, 8), pl.ds(136, 8)
+        first, last = pl.ds(0, 8), pl.ds(size - 8, 8)
+        below, middle, above = pl.ds(0, 8), pl.ds(8, size), pl.ds(8 + size, 8)
         plan = (
-            (None, pk, pw.at[pl.ds(8, 128)], la, east),
-            (None, pk, pe.at[pl.ds(8, 128)], la, west),
+            (None, se, pw.at[middle], la, east),
+            (None, sw, pe.at[middle], la, west),
             (has_north, sn, hs, north, lo),
-            (has_north, high, pw.at[below], north, east),
-            (has_north, high, pe.at[below], north, west),
+            (has_north, se.at[last], pw.at[below], north, east),
+            (has_north, sw.at[last], pe.at[below], north, west),
             (has_south, ss, hn, south, lo),
-            (has_south, low, pw.at[above], south, east),
-            (has_south, low, pe.at[above], south, west),
+            (has_south, se.at[first], pw.at[above], south, east),
+            (has_south, sw.at[first], pe.at[above], south, west),
         )
         return [
             (
@@ -191,27 +203,30 @@
             pl.when(cond)(action)
 
     def halo_start(group, bufs, source):
-        ss, sn, hs, hn, pk, pw, pe = bufs
-        count = ss.shape[0]
+        ss, sn, hs, hn, se, sw, pw, pe = bufs
+        count, size = ss.shape[0], se.shape[0]
         for n in range(count):
-            ss[n] = source(n)[pl.ds(0, 8), :]
-            sn[n] = source(n)[pl.ds(120, 8), :]
-        lane = lanes_of((NT, 128))
-        packed = jnp.zeros((NT, 128), F32)
-        for n in range(count):
-            for par in range(2):
-                j = 2 * n + par
-                value = source(n)[:, pl.ds(128 * par, 128)]
-                first = value if j == 0 else pltpu.roll(value, 4 * j, 1)
-                last = pltpu.roll(value, (4 * j - 60) % 128, 1)
-                packed = jnp.where((lane >= 4 * j) & (lane < 4 * j + 4), first, packed)
-                packed = jnp.where((lane >= 64 + 4 * j) & (lane < 68 + 4 * j), last, packed)
-        pk[...] = packed
+            ss[n] = source(n)[pl.ds(0, 2), :]
+            sn[n] = source(n)[pl.ds(126, 2), :]
+        lane = lanes_of((size, 128))
+        to_east = jnp.zeros((size, 128), F32)
+        to_west = to_east
+        for g in range(NT // size):
+            for n in range(count):
+                for par in range(2):
+                    at = 8 * count * g + 8 * n + 4 * par
+                    value = source(n)[pl.ds(size * g, size), pl.ds(128 * par, 128)]
+                    here = (lane >= at) & (lane < at + 4)
+                    to_west = jnp.where(here, pltpu.roll(value, at, 1) if at else value, to_west)
+                    to_east = jnp.where(here, pltpu.roll(value, (at - 124) % 128, 1) if at != 124 else value, to_east)
+        se[...] = to_east
+        sw[...] = to_west
         for cond, copy in halo_copies(group, bufs):
             under(cond, copy.start)
 
     def halo_walls(bufs):
-        ss, sn, hs, hn, pk, pw, pe = bufs
+        ss, sn, hs, hn, se, sw, pw, pe = bufs
+        size = se.shape[0]
         zero = jnp.zeros((8, 128), F32)
 
         @pl.when(la == 0)
@@ -223,27 +238,34 @@
         @pl.when(la == NLAT - 1)
         def _():
             hn[...] = jnp.zeros(hn.shape, F32)
-            pw[pl.ds(136, 8), :] = zero
-            pe[pl.ds(136, 8), :] = zero
+            pw[pl.ds(8 + size, 8), :] = zero
+            pe[pl.ds(8 + size, 8), :] = zero
 
     def halo_finish(group, bufs, channels, source, put):
-        ss, sn, hs, hn, pk, pw, pe = bufs
+        ss, sn, hs, hn, se, sw, pw, pe = bufs
+        count, size = ss.shape[0], se.shape[0]
         copies = halo_copies(group, bufs)
         received = {2: has_south, 3: has_south, 4: has_south, 5: has_north, 6: has_north, 7: has_north}
         for n, (cond, copy) in enumerate(copies):
             under(received.get(n), copy.wait_recv)
-        lane = lanes_of((144, 128))
-        from_west = pw[...]
-        from_east = pe[...]
+        groups = NT // size
+        parts = [(TOP + size * g, size, 8, g) for g in range(groups)]
+        parts += [(8, 8, 0, groups - 1), (TOP + NT, 8, 8 + size, 0)]
+        for start, rows, at, g in parts:
+            from_west = pw[pl.ds(at, rows), :]
+            from_east = pe[pl.ds(at, rows), :]
+            lane = lanes_of((rows, 128))
+            for n, channel in enumerate(channels):
+                for par in range(2):
+                    j = 8 * count * g + 8 * n + 4 * par
+                    right = pltpu.roll(from_east, 128 - j, 1) if j else from_east
+                    left = pltpu.roll(from_west, 124 - j, 1) if j != 124 else from_west
+                    put(channel, par, pl.ds(start, rows), pl.ds(128, 128), jnp.where(lane < 64, right, left))
         for n, channel in enumerate(channels):
             for par in range(2):
-                j = 2 * n + par
                 lanes = pl.ds(128 * par, 128)
-                right = from_east if j == 0 else pltpu.roll(from_east, 128 - 4 * j, 1)
-                left = pltpu.roll(from_west, (60 - 4 * j) % 128, 1)
-                put(channel, par, pl.ds(8, 144), pl.ds(128, 128), jnp.where(lane < 64, right, left))
-                put(channel, par, pl.ds(8, 8), pl.ds(0, 128), hs[n, :, lanes])
-                put(channel, par, pl.ds(144, 8), pl.ds(0, 128), hn[n, :, lanes])
+                put(channel, par, pl.ds(TOP - 2, 2), pl.ds(0, 128), hs[n, :, lanes])
+                put(channel, par, pl.ds(TOP + NT, 2), pl.ds(0, 128), hn[n, :, lanes])
                 put(channel, par, pl.ds(TOP, NT), pl.ds(0, 128), source(n)[:, lanes])
 
     def put_x(channel, par, rows, lanes, value):
@@ -258,14 +280,16 @@
         for cond, copy in halo_copies(group, bufs):
             under(cond, copy.wait_send)
 
-    ice_bufs = (ss1, sn1, hs1, hn1, pk1, pw1, pe1)
-    cur_bufs = (ss2, sn2, hs2, hn2, pk2, pw2, pe2)
-    push_bufs = (ss3, sn3, hs3, hn3, pk3, pw3, pe3)
+    ice_bufs = (ss1, sn1, hs1, hn1, se1, sw1, pw1, pe1)
+    cur_bufs = (ss2, sn2, hs2, hn2, se2, sw2, pw2, pe2)
+    push_bufs = (ss3, sn3, hs3, hn3, se3, sw3, pw3, pe3)
 
     @pl.when(comp == 1)
     def _():
         for load in loads:
             load.start()
+        rb[...] = jnp.zeros(rb.shape, F32)
+        rd[...] = jnp.zeros(rd.shape, F32)
         greet(0)
         greet(1)
         for load in loads:
@@ -280,8 +304,6 @@
 
         pl.semaphore_wait(barrier, 2 * NT)
 
-        others = [lax.rem(lo + j, NLON) for j in range(NLON)]
-
         def tell_one(tla, tlo):
             pltpu.make_async_remote_copy(
                 src_ref=own_ref, dst_ref=ids.at[me], send_sem=id_send, recv_sem=id_recv,
@@ -324,9 +346,9 @@
             moved = to_slots(value)
             for par in range(2):
                 sa2[pl.ds(2 * ch + par, NT, stride=4), :] = moved[:, 128 * par : 128 * par + 128]
-        for chunk in range(4):
+        for chunk in range(1, 4):
             send_chunk(sa, ra, sa_sem, ra_sem, chunk, 0)
-
+        send_chunk(sa, ra, sa_sem, ra_sem, 0, 0, 4, 2)
         halo_finish(0, ice_bufs, GROUP_ICE, ice_source, put_x)
 
         def prepare(k, carry):
@@ -417,11 +439,18 @@
 
         subcycle(True)
 
-        for chunk in range(4):
+        wait_chunk(rd, rd_sem, 0, 8)
+        for par in range(2):
+            lanes = pl.ds(128 * par, 128)
+            for ch in range(2):
+                stress_of_air = to_blocks(rd2[pl.ds(2 * ch + par, NT, stride=8), :])
+                tilt = to_blocks(rd2[pl.ds(4 + 2 * ch + par, NT, stride=8), :])
+                gat[2 + ch, :, lanes] = act[:, lanes] * (f_ref[3, :, lanes] * stress_of_air - f_ref[2, :, lanes] * tilt)
+        for chunk in range(1, 4):
             wait_chunk(rb, rb_sem, chunk)
         for ch in range(2):
             for par in range(2):
-                gat[2 + ch, :, pl.ds(128 * par, 128)] = to_blocks(rb2[pl.ds(2 * ch + par, NT, stride=4), :])
+                gat[2 + ch, :, pl.ds(128 * par, 128)] += to_blocks(rb2[pl.ds(2 * ch + par, NT, stride=4), :])
         halo_start(2, push_bufs, lambda n: gat.at[2 + n])
         halo_finish(2, push_bufs, GROUP_PUSH, lambda n: gat.at[2 + n], put_push)
 
@@ -445,19 +474,16 @@
         wait_bytes(ids.at[pl.ds(0, NT - 1)], id_send)
         for group, bufs in enumerate((ice_bufs, cur_bufs, push_bufs)):
             halo_sent(group, bufs)
-        wait_bytes(sa, sa_sem)
+        wait_bytes(sa.at[pl.ds(0, 448)], sa_sem)
         wait_bytes(sb, sb_sem)
 
 
 def halo_scratch(count):
+    size = 16 * count // 2
     return [
-        pltpu.VMEM((count, 8, 256), F32),
-        pltpu.VMEM((count, 8, 256), F32),
-        pltpu.VMEM((count, 8, 256), F32),
-        pltpu.VMEM((count, 8, 256), F32),
-        pltpu.VMEM((128, 128), F32),
-        pltpu.VMEM((144, 128), F32),
-        pltpu.VMEM((144, 128), F32),
+        *[pltpu.VMEM((count, 2, 256), F32)] * 4,
+        *[pltpu.VMEM((size, 128), F32)] * 2,
+        *[pltpu.VMEM((size + 16, 128), F32)] * 2,
     ]
 
 
@@ -475,6 +501,7 @@
             pltpu.SemaphoreType.DMA((4,)),
             pltpu.VMEM((NT, 1, NT), jnp.int32),
             *[pltpu.VMEM((4 * NT, 1, 128), F32)] * 4,
+            *[pltpu.VMEM((8 * NT, 1, 128), F32)] * 2,
             pltpu.VMEM((28, ROWS, 256), F32),
             pltpu.VMEM((NT, 256), F32),
             pltpu.VMEM((4, NT, 256), F32),
@@ -490,6 +517,8 @@
             pltpu.SemaphoreType.DMA((4,)),
             pltpu.SemaphoreType.DMA,
             pltpu.SemaphoreType.DMA((4,)),
+            pltpu.SemaphoreType.DMA,
+            pltpu.SemaphoreType.DMA((4,)),
             pltpu.SemaphoreType.DMA((24,)),
             pltpu.SemaphoreType.DMA((24,)),
         ],

time: 76.8 us -> 69.7 us (0.908); the launches traced: 75.3 us -> 69.5 us
  Pallas kernels: 73.6 us -> 67.8 us
    pallas_call x1, Pallas kernels: 73.6 us -> 67.8 us  [per_device(): pl.pallas_call(kernel, out_shape=jax.ShapeDtypeStruct((2, NT, 256), F32),...]
where the time goes in v3:
time: 69.7 us; the launch traced here: 69.5 us
  Pallas kernels  67.8 us (97%)
  local copies, waits for them, and re-layouts  1.67 us (2%)
    pallas_call x1, Pallas kernels, per_device(): pl.pallas_call(kernel, out_shape=jax.ShapeDtypeStruct((2, NT, 256), F32),...  67.8 us
    unnamed x1, local copies, waits for them, and re-layouts  1.67 us

profile of v3, /device:TPU:65, one launch (start us, length us, event | category | flops | bytes accessed | tf_op | source)
XLA Modules:
  0.0 69.5 jit_solution(17191208192252058091)
XLA Ops:
  0.0 67.8 %shard_map.46 = f32[2,128,256]{2,1,0:T(8,128)} custom-call(f32[7,128,256]{2,1,0:T(8,128)} %bitcast.5, s32[1,128]{1,0:T(1,128)} %bitcast.6, s32[1,128]{1,0:T(1,128)} %bitcast.7, s32[128,256]{1,0:T(8,128)} %land_hbm.1), custom_call_target="tpu_custom_call" | custom-call | tf_op jit(solution)/shard_map/pallas_call | solution.py:491
  67.8 1.7 %copy.6 = f32[1,2,128,256]{3,2,1,0:T(8,128)} copy(f32[1,2,128,256]{3,2,1,0:T(8,128)} %bitcast.4) | data formatting | bytes 524288

commit v4 on v3

v4 whole, which is shorter than its diff:
```python
import functools

import jax
import jax.numpy as jnp
from jax import lax
from jax.experimental import pallas as pl
from jax.experimental.pallas import tpu as pltpu
from jax.sharding import PartitionSpec as P


NSUB = 4
NLAT = 8
NLON = 16
NT = NLAT * NLON
TOP = 16
ROWS = 160
MESH = pl.DeviceIdType.MESH
HIGHEST = lax.Precision.HIGHEST
F32 = jnp.float32

U, V, S1, S2, S12, STR, MASS, DRAG, ACT, CX, CY, PX, PY, DEN, TURN = range(15)
DIRECT = 2
GROUP_ICE = (U, V, MASS, DRAG, S1, S2, S12, ACT)
GROUP_SEA = (CX, CY, PX, PY)


def lanes_of(shape):
    return lax.broadcasted_iota(jnp.int32, shape, len(shape) - 1)


def root(x):
    return x * lax.rsqrt(x)


def kernel(
    f_hbm, own_hbm, cov_hbm, land_hbm, out_ref,
    f_ref, own_ref, cov_ref, land_ref, in_sem,
    ids, sa, ra, sb, rb, sd, rd, x, act, gat, opn, outb, qmat,
    ss1, sn1, hs1, hn1, se1, sw1, pw1, pe1,
    ss2, sn2, hs2, hn2, se2, sw2, pw2, pe2,
    id_send, id_recv, sa_sem, ra_sem, sb_sem, rb_sem, sd_sem, rd_sem, h_send, h_recv,
):
    comp = lax.axis_index("comp")
    la = lax.axis_index("lat")
    lo = lax.axis_index("lon")
    me = la * NLON + lo
    barrier = pltpu.get_barrier_semaphore()
    sa2, ra2, sb2, rb2 = (r.reshape(4 * NT, 128) for r in (sa, ra, sb, rb))
    sd2, rd2 = (r.reshape(8 * NT, 128) for r in (sd, rd))

    loads = [
        pltpu.make_async_copy(src, dst, in_sem.at[n])
        for n, (src, dst) in enumerate(
            ((f_hbm, f_ref), (own_hbm, own_ref), (cov_hbm, cov_ref), (land_hbm, land_ref))
        )
    ]

    def greet(other):
        for tla in range(NLAT):
            for tlo in range(NLON):
                pl.semaphore_signal(barrier, inc=1, device_id=(other, tla, tlo), device_id_type=MESH)

    others = [lax.rem(lo + j, NLON) for j in range(NLON)]

    def target_lat(chunk, other):
        return lax.rem(la + (NLAT - chunk if other == 1 else chunk), NLAT)

    def send_chunk(src, dst, send_sem, recv_sem, chunk, other, stride=4, rows=4):
        tla = target_lat(chunk, other)
        for tlo in others:
            pltpu.make_async_remote_copy(
                src_ref=src.at[pl.ds(stride * (tla * NLON + tlo), rows)],
                dst_ref=dst.at[pl.ds(stride * me, rows)],
                send_sem=send_sem,
                recv_sem=recv_sem.at[chunk],
                device_id=(other, tla, tlo),
                device_id_type=MESH,
            ).start()

    def wait_bytes(ref, sem):
        pltpu.make_async_copy(ref, ref, sem).wait()

    def wait_chunk(dst, recv_sem, chunk, rows=4):
        wait_bytes(dst.at[pl.ds(0, NLON * rows)], recv_sem.at[chunk])

    def rows_of(chunk, half):
        return pl.multiple_of(target_lat(chunk, 1) * NLON + 8 * half, 8)

    @pl.when(comp == 0)
    def _():
        loads[0].start()
        greet(1)
        loads[0].wait()
        for ch in range(2):
            for par in range(2):
                sa2[pl.ds(2 * ch + par, NT, stride=4), :] = f_ref[2 + ch, :, pl.ds(128 * par, 128)]
        def air(k, carry):
            rows = pl.ds(pl.multiple_of(8 * k, 8), 8)
            wx, wy, cx, cy, rho = (f_ref[i, rows, :] for i in (0, 1, 2, 3, 6))
            scale = rho * 0.1 * root(wx * wx + wy * wy + 1.0)
            outb[0, rows, :] = scale * wx
            outb[1, rows, :] = scale * wy
            rx = wx - cx
            ry = wy - cy
            speed = root(rx * rx + ry * ry + 1.0)
            scale = rho * (0.1 + 0.05 * speed) * speed
            opn[0, rows, :] = scale * rx
            opn[1, rows, :] = scale * ry
            return carry

        lax.fori_loop(0, 16, air, 0)


        for chunk in range(DIRECT):
            for half in range(2):
                base = rows_of(chunk, half)
                for par in range(2):
                    lanes = pl.ds(128 * par, 128)
                    for ch in range(2):
                        sd2[pl.ds(8 * base + 2 * ch + par, 8, stride=8), :] = outb[ch, pl.ds(base, 8), lanes]
                        sd2[pl.ds(8 * base + 4 + 2 * ch + par, 8, stride=8), :] = f_ref[4 + ch, pl.ds(base, 8), lanes]

        pl.semaphore_wait(barrier, NT)
        for chunk in range(NLAT):
            send_chunk(sa, ra, sa_sem, ra_sem, chunk, 1)
        for chunk in range(DIRECT):
            send_chunk(sd, rd, sd_sem, rd_sem, chunk, 1, 8, 8)

        for chunk in range(DIRECT, NLAT):
            wait_chunk(ra, ra_sem, chunk)

            for half in range(2):
                base = rows_of(chunk, half)
                rows = pl.ds(base, 8)
                for par in range(2):
                    lanes = pl.ds(128 * par, 128)
                    conc = ra2[pl.ds(4 * base + par, 8, stride=4), :]
                    mass = ra2[pl.ds(4 * base + 2 + par, 8, stride=4), :]
                    for ch in range(2):
                        sb2[pl.ds(4 * base + 2 * ch + par, 8, stride=4), :] = (
                            conc * outb[ch, rows, lanes] - mass * f_ref[4 + ch, rows, lanes]
                        )
            send_chunk(sb, rb, sb_sem, rb_sem, chunk, 1)

        for chunk in range(NLAT):
            wait_chunk(rb, rb_sem, chunk)
        for chunk in range(DIRECT):
            wait_chunk(ra, ra_sem, chunk, 2)
        for ch in range(2):
            for par in range(2):
                lanes = pl.ds(128 * par, 128)
                conc = ra2[pl.ds(par, NT, stride=4), :]
                out_ref[ch, :, lanes] = rb2[pl.ds(2 * ch + par, NT, stride=4), :] + (1.0 - conc) * opn[ch, :, lanes]
        wait_bytes(sa, sa_sem)
        wait_bytes(sb.at[pl.ds(0, 4 * NLON * (NLAT - DIRECT))], sb_sem)
        wait_bytes(sd.at[pl.ds(0, 8 * NLON * DIRECT)], sd_sem)

    east = lax.rem(lo + 1, NLON)
    west = lax.rem(lo + NLON - 1, NLON)
    has_south = la > 0
    has_north = la < NLAT - 1

    def halo_copies(group, bufs):
        ss, sn, hs, hn, se, sw, pw, pe = bufs
        size = se.shape[0]
        south, north = la - 1, la + 1
        first, last = pl.ds(0, 8), pl.ds(size - 8, 8)
        below, middle, above = pl.ds(0, 8), pl.ds(8, size), pl.ds(8 + size, 8)
        plan = (
            (None, se, pw.at[middle], la, east),
            (None, sw, pe.at[middle], la, west),
            (has_north, sn, hs, north, lo),
            (has_north, se.at[last], pw.at[below], north, east),
            (has_north, sw.at[last], pe.at[below], north, west),
            (has_south, ss, hn, south, lo),
            (has_south, se.at[first], pw.at[above], south, east),
            (has_south, sw.at[first], pe.at[above], south, west),
        )
        return [
            (
                cond,
                pltpu.make_async_remote_copy(
                    src_ref=src, dst_ref=dst, send_sem=h_send.at[8 * group + n], recv_sem=h_recv.at[8 * group + n],
                    device_id=(1, tla, tlo), device_id_type=MESH,
                ),
            )
            for n, (cond, src, dst, tla, tlo) in enumerate(plan)
        ]

    def under(cond, action):
        if cond is None:
            action()
        else:
            pl.when(cond)(action)

    def halo_start(group, bufs, source):
        ss, sn, hs, hn, se, sw, pw, pe = bufs
        count, size = ss.shape[0], se.shape[0]
        for n in range(count):
            ss[n] = source(n)[pl.ds(0, 2), :]
            sn[n] = source(n)[pl.ds(126, 2), :]
        lane = lanes_of((size, 128))
        to_east = jnp.zeros((size, 128), F32)
        to_west = to_east
        for g in range(NT // size):
            for n in range(count):
                for par in range(2):
                    at = 8 * count * g + 8 * n + 4 * par
                    value = source(n)[pl.ds(size * g, size), pl.ds(128 * par, 128)]
                    here = (lane >= at) & (lane < at + 4)
                    to_west = jnp.where(here, pltpu.roll(value, at, 1) if at else value, to_west)
                    to_east = jnp.where(here, pltpu.roll(value, (at - 124) % 128, 1) if at != 124 else value, to_east)
        se[...] = to_east
        sw[...] = to_west
        for cond, copy in halo_copies(group, bufs):
            under(cond, copy.start)

    def halo_walls(bufs):
        ss, sn, hs, hn, se, sw, pw, pe = bufs
        size = se.shape[0]
        zero = jnp.zeros((8, 128), F32)

        @pl.when(la == 0)
        def _():
            hs[...] = jnp.zeros(hs.shape, F32)
            pw[pl.ds(0, 8), :] = zero
            pe[pl.ds(0, 8), :] = zero

        @pl.when(la == NLAT - 1)
        def _():
            hn[...] = jnp.zeros(hn.shape, F32)
            pw[pl.ds(8 + size, 8), :] = zero
            pe[pl.ds(8 + size, 8), :] = zero

    def halo_main(channels, source):
        for n, channel in enumerate(channels):
            for par in range(2):
                x[2 * channel + par, pl.ds(TOP, NT), pl.ds(0, 128)] = source(n)[:, pl.ds(128 * par, 128)]

    def halo_finish(group, bufs, channels):
        ss, sn, hs, hn, se, sw, pw, pe = bufs
        count, size = ss.shape[0], se.shape[0]
        copies = halo_copies(group, bufs)
        received = {2: has_south, 3: has_south, 4: has_south, 5: has_north, 6: has_north, 7: has_north}
        for n, (cond, copy) in enumerate(copies):
            under(received.get(n), copy.wait_recv)
        groups = NT // size
        parts = [(TOP + size * g, size, 8, g) for g in range(groups)]
        parts += [(8, 8, 0, groups - 1), (TOP + NT, 8, 8 + size, 0)]
        for start, rows, at, g in parts:
            from_west = pw[pl.ds(at, rows), :]
            from_east = pe[pl.ds(at, rows), :]
            lane = lanes_of((rows, 128))
            for n, channel in enumerate(channels):
                for par in range(2):
                    j = 8 * count * g + 8 * n + 4 * par
                    right = pltpu.roll(from_east, 128 - j, 1) if j else from_east
                    left = pltpu.roll(from_west, 124 - j, 1) if j != 124 else from_west
                    x[2 * channel + par, pl.ds(start, rows), pl.ds(128, 128)] = jnp.where(lane < 64, right, left)
        for n, channel in enumerate(channels):
            for par in range(2):
                lanes = pl.ds(128 * par, 128)
                x[2 * channel + par, pl.ds(TOP - 2, 2), pl.ds(0, 128)] = hs[n, :, lanes]
                x[2 * channel + par, pl.ds(TOP + NT, 2), pl.ds(0, 128)] = hn[n, :, lanes]

    def halo_sent(group, bufs):
        for cond, copy in halo_copies(group, bufs):
            under(cond, copy.wait_send)

    ice_bufs = (ss1, sn1, hs1, hn1, se1, sw1, pw1, pe1)
    sea_bufs = (ss2, sn2, hs2, hn2, se2, sw2, pw2, pe2)

    @pl.when(comp == 1)
    def _():
        for load in loads:
            load.start()
        rb[...] = jnp.zeros(rb.shape, F32)
        rd[...] = jnp.zeros(rd.shape, F32)
        greet(0)
        greet(1)
        for load in loads:
            load.wait()
        square = (NT, NT)
        diagonal = lax.broadcasted_iota(jnp.int32, square, 0) == lanes_of(square)
        covered = jnp.sum(jnp.where(diagonal, cov_ref[...].astype(F32), 0.0), axis=1, keepdims=True)
        act[...] = covered * (1 - land_ref[...]).astype(F32)
        halo_walls(ice_bufs)
        halo_walls(sea_bufs)

        pl.semaphore_wait(barrier, 2 * NT)

        def tell_one(tla, tlo):
            pltpu.make_async_remote_copy(
                src_ref=own_ref, dst_ref=ids.at[me], send_sem=id_send, recv_sem=id_recv,
                device_id=(1, tla, tlo), device_id_type=MESH,
            ).start()

        for tlo in others[1:]:
            tell_one(la, tlo)

        def tell(k, carry):
            tla = lax.rem(la + k, NLAT)
            for tlo in others:
                tell_one(tla, tlo)
            return carry

        lax.fori_loop(1, NLAT, tell, 0)
        ids[me] = own_ref[...]

        def ice_source(n):
            return f_ref.at[n] if n < 7 else act

        halo_start(0, ice_bufs, ice_source)

        wait_bytes(ids.at[pl.ds(0, NT - 1)], id_recv)
        every = ids.reshape(NT, NT)[...]
        local = jnp.where(lanes_of(square) == me, (every - NT * me).astype(F32), 0.0)
        local = jnp.sum(local, axis=1, keepdims=True)
        q = (local == lanes_of(square).astype(F32)).astype(F32)
        qmat[0] = q
        qmat[1] = q.T

        def to_slots(values):
            return jnp.dot(qmat[0], values, precision=HIGHEST, preferred_element_type=F32)

        def to_blocks(values):
            return jnp.dot(qmat[1], values, precision=HIGHEST, preferred_element_type=F32)

        a = act[...]
        for ch, value in enumerate((f_ref[3] * a, f_ref[2] * a)):
            moved = to_slots(value)
            for par in range(2):
                sa2[pl.ds(2 * ch + par, NT, stride=4), :] = moved[:, 128 * par : 128 * par + 128]
        for chunk in range(DIRECT, NLAT):
            send_chunk(sa, ra, sa_sem, ra_sem, chunk, 0)
        for chunk in range(DIRECT):
            send_chunk(sa, ra, sa_sem, ra_sem, chunk, 0, 4, 2)
        halo_main(GROUP_ICE, ice_source)
        halo_finish(0, ice_bufs, GROUP_ICE)

        def prepare(k, carry):
            rows = pl.ds(pl.multiple_of(48 * k + 8, 8), 48)
            for par in range(2):
                conc = x[2 * DRAG + par, rows, :]
                active = x[2 * ACT + par, rows, :]
                mass = x[2 * MASS + par, rows, :]
                x[2 * STR + par, rows, :] = mass * jnp.exp(2.0 * (conc - 1.0)) * (active * (1.0 / 6.0))
                x[2 * DRAG + par, rows, :] = 1.5 * conc * active
                x[2 * DEN + par, rows, :] = 2.0 * jnp.maximum(mass, 0.5)
                x[2 * TURN + par, rows, :] = 0.3 * mass
                x[2 * MASS + par, rows, :] = 2.0 * mass
                one = 0.5 * x[2 * S1 + par, rows, :]
                two = 0.5 * x[2 * S2 + par, rows, :]
                x[2 * S1 + par, rows, :] = one + two
                x[2 * S2 + par, rows, :] = one - two
            return carry

        lax.fori_loop(0, 3, prepare, 0)

        third = 1.0 / 1.5
        both = pl.ds(0, 256)

        def stress():
            for r in (8, 80):
                for par in range(2):
                    def get(channel, p=par, row=r):
                        return x[2 * channel + p, pl.ds(row, 72), :]

                    u, v = get(U), get(V)
                    un, vn = (get(c, 1) if par == 0 else get(c, 0, r + 1) for c in (U, V))
                    sxx = pltpu.roll(u, 255, 1) - u
                    syy = vn - v
                    shear = (un - u) + (pltpu.roll(v, 255, 1) - v)
                    div = sxx + syy
                    ten = sxx - syy
                    strength = get(STR)
                    visc = strength * lax.rsqrt(div * div + (ten * ten + shear * shear + 1.0) * 0.25)
                    quarter = 0.25 * visc
                    total = visc * div - strength
                    differ = quarter * ten
                    rows = pl.ds(r, 72)
                    x[2 * S1 + par, rows, :] = get(S1) * third + (total + differ)
                    x[2 * S2 + par, rows, :] = get(S2) * third + (total - differ)
                    x[2 * S12 + par, rows, :] = get(S12) * third + quarter * shear

        def momentum(r, n, half, final=False):
            lanes = both if half is None else pl.ds(128 * half, 128)
            for par in range(2):
                def get(channel, p=par, row=r, where=lanes):
                    return x[2 * channel + p, pl.ds(row, n), where]

                def west_of(channel):
                    rolled = pltpu.roll(get(channel), 1, 1)
                    if half is None:
                        return rolled
                    beyond = pltpu.roll(get(channel, where=pl.ds(128 - 128 * half, 128)), 1, 1)
                    return jnp.where(lanes_of((n, 128)) == 0, beyond, rolled)

                s12 = get(S12)
                south = (1, r - 1) if par == 0 else (0, r)
                force_x = get(S1) - west_of(S1) + (s12 - get(S12, *south))
                force_y = s12 - west_of(S12) + (get(S2) - get(S2, *south))
                u, v, cx, cy, mass2, turn = (get(c) for c in (U, V, CX, CY, MASS, TURN))
                dx = cx - u
                dy = cy - v
                base = get(DRAG)
                drag = base * root(dx * dx + dy * dy + 0.1)
                scale = get(ACT) / (get(DEN) + drag)
                unew = scale * (mass2 * u + force_x + get(PX) + drag * cx + turn * v)
                vnew = scale * (mass2 * v + force_y + get(PY) + drag * cy - turn * u)
                if final:
                    rows, place = pl.ds(r - TOP, n), pl.ds(128 * par, 128)
                    out_ref[0, rows, place] = unew
                    out_ref[1, rows, place] = vnew
                    dx = unew - cx
                    dy = vnew - cy
                    factor = base * root(dx * dx + dy * dy + 0.1)
                    gat[0, rows, place] = factor * dx
                    gat[1, rows, place] = factor * dy
                else:
                    x[2 * U + par, pl.ds(r, n), lanes] = unew
                    x[2 * V + par, pl.ds(r, n), lanes] = vnew

        stress()

        for chunk in range(NLAT):
            wait_chunk(ra, ra_sem, chunk)
        for ch in range(2):
            for par in range(2):
                gat[ch, :, pl.ds(128 * par, 128)] = to_blocks(ra2[pl.ds(2 * ch + par, NT, stride=4), :])
        for chunk in range(DIRECT):
            wait_chunk(rd, rd_sem, chunk, 8)
        for par in range(2):
            lanes = pl.ds(128 * par, 128)
            for ch in range(2):
                stress_of_air = to_blocks(rd2[pl.ds(2 * ch + par, NT, stride=8), :])
                tilt = to_blocks(rd2[pl.ds(4 + 2 * ch + par, NT, stride=8), :])
                gat[2 + ch, :, lanes] = act[:, lanes] * (f_ref[3, :, lanes] * stress_of_air - f_ref[2, :, lanes] * tilt)
        for chunk in range(DIRECT, NLAT):
            wait_chunk(rb, rb_sem, chunk)
        for ch in range(2):
            for par in range(2):
                gat[2 + ch, :, pl.ds(128 * par, 128)] += to_blocks(rb2[pl.ds(2 * ch + par, NT, stride=4), :])
        halo_start(1, sea_bufs, lambda n: gat.at[n])
        halo_main(GROUP_SEA, lambda n: gat.at[n])
        momentum(TOP, 64, 0)
        momentum(TOP + 64, 64, 0)
        halo_finish(1, sea_bufs, GROUP_SEA)
        momentum(8, 8, 0)
        momentum(TOP + NT, 8, 0)
        momentum(8, 144, 1)
        for repeat in range(NSUB - 2):
            stress()
            momentum(8, 72, None)
            momentum(80, 72, None)
        stress()
        momentum(TOP, 64, 0, True)
        momentum(TOP + 64, 64, 0, True)
        for ch in range(2):
            for par in range(2):
                sb2[pl.ds(2 * ch + par, NT, stride=4), :] = to_slots(gat[ch, :, pl.ds(128 * par, 128)])
        for chunk in range(NLAT):
            send_chunk(sb, rb, sb_sem, rb_sem, chunk, 0)
        wait_bytes(ids.at[pl.ds(0, NT - 1)], id_send)
        for group, bufs in enumerate((ice_bufs, sea_bufs)):
            halo_sent(group, bufs)
        wait_bytes(sa.at[pl.ds(0, 4 * NT - 2 * NLON * DIRECT)], sa_sem)
        wait_bytes(sb, sb_sem)


def halo_scratch(count):
    size = 16 * count // 2
    return [
        *[pltpu.VMEM((count, 2, 256), F32)] * 4,
        *[pltpu.VMEM((size, 128), F32)] * 2,
        *[pltpu.VMEM((size + 16, 128), F32)] * 2,
    ]


def per_device(fields, block_owner, ice_covered, land_mask):
    out = pl.pallas_call(
        kernel,
        out_shape=jax.ShapeDtypeStruct((2, NT, 256), F32),
        in_specs=[pl.BlockSpec(memory_space=pltpu.HBM)] * 4,
        out_specs=pl.BlockSpec(memory_space=pltpu.VMEM),
        scratch_shapes=[
            pltpu.VMEM((7, NT, 256), F32),
            pltpu.VMEM((1, NT), jnp.int32),
            pltpu.VMEM((1, NT), jnp.int32),
            pltpu.VMEM((NT, 256), jnp.int32),
            pltpu.SemaphoreType.DMA((4,)),
            pltpu.VMEM((NT, 1, NT), jnp.int32),
            *[pltpu.VMEM((4 * NT, 1, 128), F32)] * 4,
            *[pltpu.VMEM((8 * NT, 1, 128), F32)] * 2,
            pltpu.VMEM((30, ROWS, 256), F32),
            pltpu.VMEM((NT, 256), F32),
            pltpu.VMEM((4, NT, 256), F32),
            pltpu.VMEM((2, NT, 256), F32),
            pltpu.VMEM((2, NT, 256), F32),
            pltpu.VMEM((2, NT, NT), F32),
            *halo_scratch(8),
            *halo_scratch(4),
            pltpu.SemaphoreType.DMA,
            pltpu.SemaphoreType.DMA,
            pltpu.SemaphoreType.DMA,
            pltpu.SemaphoreType.DMA((NLAT,)),
            pltpu.SemaphoreType.DMA,
            pltpu.SemaphoreType.DMA((NLAT,)),
            pltpu.SemaphoreType.DMA,
            pltpu.SemaphoreType.DMA((NLAT,)),
            pltpu.SemaphoreType.DMA((16,)),
            pltpu.SemaphoreType.DMA((16,)),
        ],
        compiler_params=pltpu.CompilerParams(
            collective_id=0, has_side_effects=True, vmem_limit_bytes=40 * 1024 * 1024
        ),
    )(
        *(
            pltpu.with_memory_space_constraint(a, pltpu.HBM)
            for a in (fields[0], block_owner.reshape(1, NT), ice_covered.reshape(1, NT), land_mask)
        )
    )
    return out[None]


def solution(mesh):
    placed = (
        P("comp", None, ("lat", "lon"), None),
        P(("lat", "lon")),
        P(("lat", "lon")),
        P(("lat", "lon"), None),
    )
    return jax.shard_map(
        per_device,
        mesh=mesh,
        in_specs=placed,
        out_specs=P("comp", None, ("lat", "lon"), None),
        check_vma=False,
    )
```

time: 69.7 us -> 64.6 us (0.927)
  Pallas kernels: 67.8 us -> 63.8 us
  local copies, waits for them, and re-layouts: 1.67 us -> 0.71 us
    pallas_call x1, Pallas kernels: 67.8 us -> 63.8 us  [per_device(): pl.pallas_call(kernel, out_shape=jax.ShapeDtypeStruct((2, NT, 256), F32),...]
    unnamed x1, local copies, waits for them, and re-layouts: 1.67 us -> 0.71 us
where the time goes in v4:
time: 64.6 us; the launch traced here: 64.5 us
  Pallas kernels  63.8 us (99%)
  local copies, waits for them, and re-layouts  0.71 us (1%)
    pallas_call x1, Pallas kernels, per_device(): pl.pallas_call(kernel, out_shape=jax.ShapeDtypeStruct((2, NT, 256), F32),...  63.8 us

profile of v4, /device:TPU:65, one launch (start us, length us, event | category | flops | bytes accessed | tf_op | source)
XLA Modules:
  0.0 64.5 jit_solution(8357646932107630272)
XLA Ops:
  0.0 63.8 %shard_map.46 = f32[2,128,256]{2,1,0:T(8,128)S(1)} custom-call(f32[7,128,256]{2,1,0:T(8,128)} %bitcast.5, s32[1,128]{1,0:T(1,128)} %bitcast.6, s32[1,128]{1,0:T(1,128)} %bitcast.7, s32[128,256]{1,0:T(8,128)} %land_hbm.1), custom_call_target="tpu_custom_call" | custom-call | tf_op jit(solution)/shard_map/pallas_call | solution.py:481
  63.8 0.7 %copy.6 = f32[1,2,128,256]{3,2,1,0:T(8,128)} copy(f32[1,2,128,256]{3,2,1,0:T(8,128)S(1)} %bitcast.4) | data formatting | bytes 524288

commit v5 on v4

--- a/solution.py
+++ b/solution.py
@@ -142,15 +142,19 @@
                         )
             send_chunk(sb, rb, sb_sem, rb_sem, chunk, 1)
 
+        for chunk in range(DIRECT):
+            wait_chunk(ra, ra_sem, chunk, 2)
         for chunk in range(NLAT):
             wait_chunk(rb, rb_sem, chunk)
-        for chunk in range(DIRECT):
-            wait_chunk(ra, ra_sem, chunk, 2)
-        for ch in range(2):
+            base = rows_of(chunk, 0)
+            rows = pl.ds(base, NLON)
             for par in range(2):
                 lanes = pl.ds(128 * par, 128)
-                conc = ra2[pl.ds(par, NT, stride=4), :]
-                out_ref[ch, :, lanes] = rb2[pl.ds(2 * ch + par, NT, stride=4), :] + (1.0 - conc) * opn[ch, :, lanes]
+                rest = 1.0 - ra2[pl.ds(4 * base + par, NLON, stride=4), :]
+                for ch in range(2):
+                    out_ref[ch, rows, lanes] = (
+                        rb2[pl.ds(4 * base + 2 * ch + par, NLON, stride=4), :] + rest * opn[ch, rows, lanes]
+                    )
         wait_bytes(sa, sa_sem)
         wait_bytes(sb.at[pl.ds(0, 4 * NLON * (NLAT - DIRECT))], sb_sem)
         wait_bytes(sd.at[pl.ds(0, 8 * NLON * DIRECT)], sd_sem)
@@ -274,10 +278,14 @@
     def _():
         for load in loads:
             load.start()
-        rb[...] = jnp.zeros(rb.shape, F32)
-        rd[...] = jnp.zeros(rd.shape, F32)
         greet(0)
         greet(1)
+        for chunk in range(NLAT):
+            first = lax.rem(la + chunk, NLAT) * NLON
+            if chunk < DIRECT:
+                rb[pl.ds(4 * first, 4 * NLON)] = jnp.zeros((4 * NLON, 1, 128), F32)
+            else:
+                rd[pl.ds(8 * first, 8 * NLON)] = jnp.zeros((8 * NLON, 1, 128), F32)
         for load in loads:
             load.wait()
         square = (NT, NT)

time: 64.6 us -> 64.2 us (level)
  no operation moved by 1% of the time
where the time goes in v5:
time: 64.2 us; the launch traced here: 64.1 us
  Pallas kernels  63.4 us (99%)
  local copies, waits for them, and re-layouts  0.71 us (1%)
    pallas_call x1, Pallas kernels, per_device(): pl.pallas_call(kernel, out_shape=jax.ShapeDtypeStruct((2, NT, 256), F32),...  63.4 us

profile of v5, /device:TPU:65, one launch (start us, length us, event | category | flops | bytes accessed | tf_op | source)
XLA Modules:
  0.0 64.1 jit_solution(15150588580985563411)
XLA Ops:
  0.0 63.4 %shard_map.46 = f32[2,128,256]{2,1,0:T(8,128)S(1)} custom-call(f32[7,128,256]{2,1,0:T(8,128)} %bitcast.5, s32[1,128]{1,0:T(1,128)} %bitcast.6, s32[1,128]{1,0:T(1,128)} %bitcast.7, s32[128,256]{1,0:T(8,128)} %land_hbm.1), custom_call_target="tpu_custom_call" | custom-call | tf_op jit(solution)/shard_map/pallas_call | solution.py:489
  63.4 0.7 %copy.6 = f32[1,2,128,256]{3,2,1,0:T(8,128)} copy(f32[1,2,128,256]{3,2,1,0:T(8,128)S(1)} %bitcast.4) | data formatting | bytes 524288

commit v6 on v5

--- a/solution.py
+++ b/solution.py
@@ -121,10 +121,10 @@
                         sd2[pl.ds(8 * base + 4 + 2 * ch + par, 8, stride=8), :] = f_ref[4 + ch, pl.ds(base, 8), lanes]
 
         pl.semaphore_wait(barrier, NT)
+        for chunk in range(DIRECT):
+            send_chunk(sd, rd, sd_sem, rd_sem, chunk, 1, 8, 8)
         for chunk in range(NLAT):
             send_chunk(sa, ra, sa_sem, ra_sem, chunk, 1)
-        for chunk in range(DIRECT):
-            send_chunk(sd, rd, sd_sem, rd_sem, chunk, 1, 8, 8)
 
         for chunk in range(DIRECT, NLAT):
             wait_chunk(ra, ra_sem, chunk)

time: 64.2 us -> 64.1 us (level)
  no operation moved by 1% of the time
where the time goes in v6:
time: 64.1 us; the launch traced here: 64 us
  Pallas kernels  63.3 us (99%)
  local copies, waits for them, and re-layouts  0.71 us (1%)
    pallas_call x1, Pallas kernels, per_device(): pl.pallas_call(kernel, out_shape=jax.ShapeDtypeStruct((2, NT, 256), F32),...  63.3 us

profile of v6, /device:TPU:65, one launch (start us, length us, event | category | flops | bytes accessed | tf_op | source)
XLA Modules:
  0.0 64.0 jit_solution(1128561159878612962)
XLA Ops:
  0.0 63.3 %shard_map.46 = f32[2,128,256]{2,1,0:T(8,128)S(1)} custom-call(f32[7,128,256]{2,1,0:T(8,128)} %bitcast.5, s32[1,128]{1,0:T(1,128)} %bitcast.6, s32[1,128]{1,0:T(1,128)} %bitcast.7, s32[128,256]{1,0:T(8,128)} %land_hbm.1), custom_call_target="tpu_custom_call" | custom-call | tf_op jit(solution)/shard_map/pallas_call | solution.py:489
  63.3 0.7 %copy.6 = f32[1,2,128,256]{3,2,1,0:T(8,128)} copy(f32[1,2,128,256]{3,2,1,0:T(8,128)S(1)} %bitcast.4) | data formatting | bytes 524288
